TPU v7x, 32 devices: a whole 2x2x4 slice. The times are simulated.
32 devices in a mesh: tiles: 2 (over x), rows: 8 (over z, y), dates: 2 (over core).
Axes of the slice: x: 2, y: 2, z: 4, core: 2. Of those that a mesh axis runs over, the one named last changes fastest.
Arguments:
- red_band: int32 [24, 512, 2048], P('dates', ('tiles', 'rows')), parts along dimension 1, may hold values from 1 to 1073741823
- nir_band: int32 [24, 512, 2048], P('dates', ('tiles', 'rows')), parts along dimension 1, may hold values from 1 to 1073741823
- cloud_class: int32 [24, 512, 2048], P('dates', ('tiles', 'rows')), parts along dimension 1, may hold values from 0 to 3
- date_ordinal: int32 [48], P(('tiles', 'dates')), parts along dimension 0, may hold values from 0 to 23, each once
Outputs:
- composite_red: int32 [512, 2048], P(('tiles', 'rows', 'dates')), parts along dimension 0
- composite_nir: int32 [512, 2048], P(('tiles', 'rows', 'dates')), parts along dimension 0
- chosen_date: int32 [512, 2048], P(('tiles', 'rows', 'dates')), parts along dimension 0
- overview_one: float32 [2, 256, 1024], P(None, ('tiles', 'rows', 'dates')), parts along dimension 1
- overview_two: float32 [2, 128, 512], P(None, ('tiles', 'rows', 'dates')), parts along dimension 1
- overview_three: float32 [2, 64, 256], P(None, ('tiles', 'rows', 'dates')), parts along dimension 1
There are 2 independent parts, one for each index of `tiles`. A program takes and returns all parts, laid end to end along the dimension named above; each array names one. Nothing has to cross between parts.
Inputs may be any that keep to these rules, and one draw needn't show every extreme that they name: `date_ordinal`: each ordinal appears once.
All inputs are finite; a program needn't handle non-finite values.
Results may differ from a plain program's by a relative error of at most 0.0003.
Values sent between devices are 32-bit elements; how exact they have to be, the bound alone decides.
A program may use at most 192 MiB of HBM per device.

v0:
```python
import functools

import jax
import jax.numpy as jnp
from jax import lax
from jax.experimental import pallas as pl
from jax.experimental.pallas import tpu as pltpu
from jax.sharding import PartitionSpec as P

LEVELS = 3
LIMB_BITS = 15
LIMB_MASK = (1 << LIMB_BITS) - 1
FLAG = 1 << 30
SCALE_BAND = 2.0**-30
LANES = 128
WIDTH = 512
PARTS = 2
MESH = pl.DeviceIdType.MESH


def taps(distance):
    far = (distance == 0) | (distance == 5)
    mid = (distance == 1) | (distance == 4)
    near = (distance == 2) | (distance == 3)
    return jnp.where(near, 0.3125, jnp.where(mid, 0.15625, jnp.where(far, 0.03125, 0.0)))


def limbs(value):
    return value >> LIMB_BITS, value & LIMB_MASK


def take_first(first, second):
    r1a, r0a, n1a, n0a, clear_a, ord_a = first
    r1b, r0b, n1b, n0b, clear_b, ord_b = second
    low = n0a * r0b - n0b * r0a + ((ord_b - ord_a) >> 31)
    mid = (n1a * r0b + n0a * r1b) - (n1b * r0a + n0b * r1a) + (low >> LIMB_BITS)
    high = n1a * r1b - n1b * r1a + (mid >> LIMB_BITS)
    return high >= clear_b - clear_a


def pick(take, first, second):
    return tuple(jnp.where(take, one, two) for one, two in zip(first, second))


def joined(entry):
    r1, r0, n1, n0, clear, order = entry
    return (r1 << LIMB_BITS) | r0, (n1 << LIMB_BITS) | n0, clear, order


def dot_split(left, right, exact_left):
    data = right if exact_left else left
    high = data.astype(jnp.bfloat16)
    low = (data - high.astype(jnp.float32)).astype(jnp.bfloat16)
    if exact_left:
        dot = lambda part: jnp.dot(left, part, preferred_element_type=jnp.float32)
    else:
        dot = lambda part: jnp.dot(part, right, preferred_element_type=jnp.float32)
    return dot(high) + dot(low)


def filter_columns(source, weights):
    rows = source.shape[0]
    blocks = (source.shape[1] - 2 * LANES) // (2 * LANES)
    left = jnp.concatenate([source[:, 2 * LANES * b : 2 * LANES * b + 4 * LANES] for b in range(blocks)], axis=0)
    out = dot_split(left, weights, False)
    return [out[b * rows : (b + 1) * rows] for b in range(blocks)]


def iota(shape, axis):
    return lax.broadcasted_iota(jnp.int32, shape, axis)


def kernel(
    red, nir, cloud, ordinals, out_red, out_nir, out_ord, out_1, out_2, out_3,
    in_red, in_nir, in_cloud, best, arrived, wide_0, ybuf, wide_1, wide_2, zbuf,
    ords, load_sem, order_sem, send_sem, recv_sem,
):
    tile = lax.axis_index("tiles")
    strip_index = lax.axis_index("rows")
    core = lax.axis_index("dates")
    strips = lax.axis_size("rows")
    dates, strip, width = red.shape
    chunk = strip // 4
    half = width // 2
    has_outer = jnp.where(core == 0, strip_index > 0, strip_index < strips - 1)
    outer_strip = jnp.clip(strip_index + 2 * core - 1, 0, strips - 1)
    partner = (tile, strip_index, 1 - core)
    outer = (tile, outer_strip, 1 - core)
    rows_of = [(3 - 3 * core) * chunk, 3 * core * chunk, (2 - core) * chunk, (1 + core) * chunk]

    loads = []
    piece = width // PARTS
    for slot, begin in enumerate(rows_of):
        begin = pl.multiple_of(begin, chunk)
        for part in range(PARTS):
            columns = pl.ds(part * piece, piece)
            group = [
                pltpu.make_async_copy(
                    source.at[:, pl.ds(begin, chunk), columns],
                    target.at[slot, :, :, columns],
                    load_sem.at[slot, part, number],
                )
                for number, (source, target) in enumerate(((red, in_red), (nir, in_nir), (cloud, in_cloud)))
            ]
            for copy in group:
                copy.start()
            loads.append(group)
    order_copy = pltpu.make_async_copy(ordinals, ords, order_sem)
    order_copy.start()

    barrier = pltpu.get_barrier_semaphore()
    pl.semaphore_signal(barrier, inc=1, device_id=partner, device_id_type=MESH)

    @pl.when(has_outer)
    def _():
        pl.semaphore_signal(barrier, inc=1, device_id=outer, device_id_type=MESH)

    k = iota((4 * LANES, LANES), 0)
    j = iota((4 * LANES, LANES), 1)
    column_weights = taps(k - LANES - (2 * j - 2)).astype(jnp.bfloat16)

    @pl.when(jnp.logical_not(has_outer))
    def _():
        ybuf[2] = jnp.zeros(ybuf.shape[1:], jnp.float32)
        zbuf[2] = jnp.zeros(zbuf.shape[1:], jnp.float32)

    for wide in (wide_0, wide_1, wide_2):
        edge = jnp.zeros((wide.shape[0], LANES), jnp.float32)
        wide[:, 0:LANES] = edge
        wide[:, wide.shape[1] - LANES :] = edge

    order_copy.wait()

    def find_best(slot, part):
        for copy in loads[slot * PARTS + part]:
            copy.wait()

        def step(number, unused):
            columns = pl.ds(pl.multiple_of(number * WIDTH + part * piece, WIDTH), WIDTH)

            def entry(date):
                red_hi, red_lo = limbs(in_red[slot, date, :, columns])
                nir_hi, nir_lo = limbs(in_nir[slot, date, :, columns])
                clear = jnp.where(in_cloud[slot, date, :, columns] == 0, FLAG, 0)
                return (red_hi, red_lo, nir_hi, nir_lo, clear, ords[date])

            current = None
            for date in range(0, dates, 2):
                other = entry(date)
                if date + 1 < dates:
                    later = entry(date + 1)
                    other = pick(take_first(later, other), later, other)
                current = other if current is None else pick(take_first(other, current), other, current)
            value_red, value_nir, clear, order = joined(current)
            best[slot, 0, :, columns] = value_red
            best[slot, 1, :, columns] = value_nir
            best[slot, 2, :, columns] = clear + order
            return unused

        lax.fori_loop(0, piece // WIDTH, step, 0)

    partner_sends = []

    def send_best(slot, place, part):
        columns = pl.ds(part * piece, piece)
        copy = pltpu.make_async_remote_copy(
            src_ref=best.at[slot, :, :, columns],
            dst_ref=arrived.at[place, :, :, columns],
            send_sem=send_sem.at[3 + place * PARTS + part],
            recv_sem=recv_sem.at[3 + place * PARTS + part],
            device_id=partner,
            device_id_type=MESH,
        )
        copy.start()
        partner_sends.append(copy)

    def wait_best(place):
        for copy in partner_sends[place * PARTS : (place + 1) * PARTS]:
            copy.wait_recv()

    def merge(slot, place, out_row):
        def step(number, unused):
            at = pl.multiple_of(number * WIDTH, WIDTH)
            columns = pl.ds(at, WIDTH)

            def entry(source):
                red_hi, red_lo = limbs(source[0, :, columns])
                nir_hi, nir_lo = limbs(source[1, :, columns])
                packed = source[2, :, columns]
                return (red_hi, red_lo, nir_hi, nir_lo, packed & FLAG, packed & (FLAG - 1))

            mine, theirs = entry(best.at[slot]), entry(arrived.at[place])
            value_red, value_nir, clear, order = joined(pick(take_first(theirs, mine), theirs, mine))
            if out_row is not None:
                rows = pl.ds(pl.multiple_of(out_row, chunk), chunk)
                out_red[rows, columns] = value_red
                out_nir[rows, columns] = value_nir
                out_ord[rows, columns] = order
            inner = pl.ds(pl.multiple_of(at + LANES, LANES), WIDTH)
            wide_0[0:chunk, inner] = value_red.astype(jnp.float32) * SCALE_BAND
            wide_0[chunk : 2 * chunk, inner] = value_nir.astype(jnp.float32) * SCALE_BAND
            return unused

        lax.fori_loop(0, width // WIDTH, step, 0)

    def columns_of(place):
        for number, block in enumerate(filter_columns(wide_0, column_weights)):
            ybuf[place, :, number * LANES : (number + 1) * LANES] = block

    for part in range(PARTS):
        find_best(0, part)
        if part == 0:
            pl.semaphore_wait(barrier, 1 + has_outer.astype(jnp.int32))
        send_best(0, 0, part)
    for part in range(PARTS):
        find_best(1, part)
    wait_best(0)
    merge(1, 0, core * chunk)
    columns_of(0)
    halo = pltpu.make_async_remote_copy(
        src_ref=ybuf.at[0],
        dst_ref=ybuf.at[2],
        send_sem=send_sem.at[0],
        recv_sem=recv_sem.at[0],
        device_id=outer,
        device_id_type=MESH,
    )

    @pl.when(has_outer)
    def _():
        halo.start()

    for slot, place in ((2, 1), (3, 2)):
        for part in range(PARTS):
            find_best(slot, part)
            send_best(slot, place, part)
    wait_best(1)
    merge(3, 1, (1 - core) * chunk)
    columns_of(1)

    quarter = chunk // 2
    def row_weights(first, count):
        shape = (4 * chunk, count * 2 * chunk)
        m = iota(shape, 0)
        band_m = m // (2 * chunk)
        within = m % (2 * chunk)
        row_1 = jnp.where(within < chunk, within, jnp.where(within < chunk + quarter, within - chunk - quarter, within - quarter))
        c = iota(shape, 1)
        place = c // (2 * chunk) + first
        band_c = (c // chunk) % 2
        from_core_0 = jnp.where(place == 2, -chunk, jnp.where(place == 3, 2 * chunk, place * chunk))
        from_core_1 = chunk - from_core_0
        row_0 = jnp.where(core == 0, from_core_0, from_core_1) + c % chunk
        from_edge = jnp.where(core == 0, row_1, chunk - 1 - row_1)
        inside = from_edge >= jnp.where(has_outer, -chunk, 0)
        return jnp.where((band_m == band_c) & inside, taps(row_0 - (2 * row_1 - 2)), 0.0).astype(jnp.bfloat16)

    rows_1a, rows_1b = row_weights(0, 3), row_weights(3, 1)

    m = iota((3 * chunk, 4 * chunk), 0)
    packed = m >= 2 * chunk
    band_m = jnp.where(packed, (m - 2 * chunk) // quarter, m // chunk)
    row_2 = jnp.where(packed, m % quarter, m % chunk)
    c = iota((3 * chunk, 4 * chunk), 1)
    band_c = c // (2 * chunk)
    within = c % (2 * chunk)
    row_1 = jnp.where(within < chunk, within, jnp.where(within < chunk + quarter, within - chunk - quarter, within - quarter))
    rows_2 = jnp.where(band_m == band_c, taps(row_1 - (2 * row_2 - 2)), 0.0).astype(jnp.bfloat16)

    m = iota((2 * chunk, 3 * chunk), 0)
    c = iota((2 * chunk, 3 * chunk), 1)
    place = c // chunk
    toward = quarter * (1 - 2 * core)
    side = jnp.where(place == 0, 0, jnp.where(place == 1, toward, -toward))
    row_2 = c % quarter + side
    rows_3 = jnp.where(m // chunk == (c % chunk) // quarter, taps(row_2 - (2 * (m % chunk) - 2)), 0.0)
    rows_3 = rows_3.astype(jnp.bfloat16)

    def next_levels(level_1):
        wide_1[:, LANES : LANES + half] = level_1
        data = jnp.concatenate(filter_columns(wide_1, column_weights), axis=1)
        level_2 = dot_split(rows_2, data, True)
        wide_2[:, LANES : LANES + half // 2] = level_2[2 * chunk :]
        return level_2, jnp.concatenate(filter_columns(wide_2, column_weights), axis=1)

    def send_z(source, slot, device):
        return pltpu.make_async_remote_copy(
            src_ref=zbuf.at[source],
            dst_ref=zbuf.at[slot],
            send_sem=send_sem.at[slot],
            recv_sem=recv_sem.at[slot],
            device_id=device,
            device_id_type=MESH,
        )

    to_partner, to_outer = send_z(0, 1, partner), send_z(3, 2, outer)

    @pl.when(has_outer)
    def _():
        halo.wait_recv()

    level_1a = dot_split(rows_1a, ybuf[0:3].reshape(6 * chunk, half), True)
    zbuf[3] = next_levels(level_1a)[1]

    @pl.when(has_outer)
    def _():
        to_outer.start()

    wait_best(2)
    merge(2, 2, None)
    columns_of(3)
    level_1 = level_1a + dot_split(rows_1b, ybuf[3], True)
    level_2, zbuf[0] = next_levels(level_1)
    to_partner.start()
    out_1[0] = level_1[0:chunk]
    out_1[1] = level_1[2 * chunk : 3 * chunk]
    out_2[0] = level_2[0:quarter]
    out_2[1] = level_2[chunk : chunk + quarter]
    to_partner.wait_recv()

    @pl.when(has_outer)
    def _():
        to_outer.wait_recv()

    level_3 = dot_split(rows_3, zbuf[0:3].reshape(3 * chunk, zbuf.shape[2]), True)
    out_3[0] = level_3[0 : quarter // 2]
    out_3[1] = level_3[chunk : chunk + quarter // 2]

    for copy in partner_sends + [to_partner]:
        copy.wait_send()

    @pl.when(has_outer)
    def _():
        halo.wait_send()
        to_outer.wait_send()


def write_out(*refs):
    count = len(refs) // 2
    semaphores = refs[-1]
    copies = [pltpu.make_async_copy(refs[n], refs[count + n], semaphores.at[n]) for n in range(count)]
    for copy in copies:
        copy.start()
    for copy in copies:
        copy.wait()


def body(red_band, nir_band, cloud_class, date_ordinal):
    dates, strip, width = red_band.shape
    own = strip // 2
    chunk = strip // 4
    whole = pl.BlockSpec(memory_space=pltpu.VMEM)
    anywhere = pl.BlockSpec(memory_space=pl.ANY)
    outs = [jax.ShapeDtypeStruct((own, width), jnp.int32)] * 3
    outs += [jax.ShapeDtypeStruct((2, own >> n, width >> n), jnp.float32) for n in range(1, LEVELS + 1)]
    kept = [pltpu.VMEM(out.shape, out.dtype) for out in outs]
    stream = pltpu.VMEM((4, dates, chunk, width), jnp.int32)
    results = pl.pallas_call(
        kernel,
        out_shape=kept,
        in_specs=[anywhere] * 4,
        out_specs=[whole] * 6,
        scratch_shapes=[
            stream,
            stream,
            stream,
            pltpu.VMEM((4, 3, chunk, width), jnp.int32),
            pltpu.VMEM((3, 3, chunk, width), jnp.int32),
            pltpu.VMEM((2 * chunk, width + 2 * LANES), jnp.float32),
            pltpu.VMEM((4, 2 * chunk, width // 2), jnp.float32),
            pltpu.VMEM((4 * chunk, width // 2 + 2 * LANES), jnp.float32),
            pltpu.VMEM((chunk, width // 4 + 2 * LANES), jnp.float32),
            pltpu.VMEM((4, chunk, width // 8), jnp.float32),
            pltpu.SMEM((dates,), jnp.int32),
            pltpu.SemaphoreType.DMA((4, PARTS, 3)),
            pltpu.SemaphoreType.DMA,
            pltpu.SemaphoreType.DMA((3 + 3 * PARTS,)),
            pltpu.SemaphoreType.DMA((3 + 3 * PARTS,)),
        ],
        compiler_params=pltpu.CompilerParams(collective_id=0, has_side_effects=True),
        name="composite",
    )(red_band, nir_band, cloud_class, date_ordinal)
    return pl.pallas_call(
        write_out,
        out_shape=outs,
        in_specs=[whole] * 6,
        out_specs=[anywhere] * 6,
        scratch_shapes=[pltpu.SemaphoreType.DMA((6,))],
        name="write_out",
    )(*[pltpu.with_memory_space_constraint(result, pltpu.VMEM) for result in results])


def solution(mesh):
    in_specs = (
        P("dates", ("tiles", "rows"), None),
        P("dates", ("tiles", "rows"), None),
        P("dates", ("tiles", "rows"), None),
        P(("tiles", "dates")),
    )
    out_specs = (
        P(("tiles", "rows", "dates"), None),
        P(("tiles", "rows", "dates"), None),
        P(("tiles", "rows", "dates"), None),
        P(None, ("tiles", "rows", "dates"), None),
        P(None, ("tiles", "rows", "dates"), None),
        P(None, ("tiles", "rows", "dates"), None),
    )
    return jax.shard_map(body, mesh=mesh, in_specs=in_specs, out_specs=out_specs, check_vma=False)
```

profile of v0, /device:TPU:0, one launch (start us, length us, event | category | flops | bytes accessed | tf_op | source)
XLA Modules:
  0.0 12.6 jit_solution(5453223259059947568)
XLA Ops:
  0.6 11.2 %composite.1 = (s32[16,2048]{1,0:T(8,128)S(1)}, s32[16,2048]{1,0:T(8,128)S(1)}, s32[16,2048]{1,0:T(8,128)S(1)}, f32[2,8,1024]{2,1,0:T(8,128)S(1)}, f32[2,4,512]{2,1,0:T(4,128)S(1)}, /*index=5*/f32[2,2,256]{2,1,0:T(2,128)S(1)}) custom-call(s32[12,32,2048]{2,1,0:T(8,128)} %red.1, s32[12,32,2048]{2,1,0:T(8,128)} %nir.1, s32[12,32,2048]{2,1,0:T(8,128)} %cloud.1, ...), custom_call_target="tpu_custom_call" | custom-call | tf_op jit(solution)/shard_map/composite/pallas_call | solution.py:358
  11.8 0.8 %write_out.1 = (s32[16,2048]{1,0:T(8,128)}, s32[16,2048]{1,0:T(8,128)}, s32[16,2048]{1,0:T(8,128)}, f32[2,8,1024]{2,1,0:T(8,128)}, f32[2,4,512]{2,1,0:T(4,128)}, /*index=5*/f32[2,2,256]{2,1,0:T(2,128)}) custom-call(s32[16,2048]{1,0:T(8,128)S(1)} %get-tuple-element.12.refs_0_, s32[16,2048]{1,0:T(8,128)S(1)} %get-tuple-element.13.refs_1_, ...), custom_call_target="tpu_custom_call" | custom-call | tf_op jit(solution)/shard_map/write_out/pallas_call | solution.py:383
where the time goes:
time: 12.8 us; the launch traced here: 12.6 us
  Pallas kernels  12 us (94%)
  between operations  0.64 us (5%)
    pallas_call x1, Pallas kernels, body(): pl.pallas_call(kernel, out_shape=kept, in_specs=[anywhere] * 4, out_specs...  11.2 us
    pallas_call x1, Pallas kernels, body(): pl.pallas_call(write_out, out_shape=outs, in_specs=[whole] * 6, out_specs...  0.82 us

commit v1 on v0

v1 whole, which is shorter than its diff:
```python
import jax
import jax.numpy as jnp
import numpy as np
from jax import lax
from jax.experimental import pallas as pl
from jax.experimental.pallas import tpu as pltpu
from jax.sharding import PartitionSpec as P

LEVELS = 3
LIMB_BITS = 15
LIMB_MASK = (1 << LIMB_BITS) - 1
FLAG = 1 << 30
SCALE_BAND = 2.0**-30
LANES = 128
TILE = 8
WIDTH = 512
MESH = pl.DeviceIdType.MESH
TAPS = np.array([1, 5, 10, 10, 5, 1], np.float64) / 32


def taps(distance):
    far = (distance == 0) | (distance == 5)
    mid = (distance == 1) | (distance == 4)
    near = (distance == 2) | (distance == 3)
    return jnp.where(near, 0.3125, jnp.where(mid, 0.15625, jnp.where(far, 0.03125, 0.0)))


def limbs(value):
    return value >> LIMB_BITS, value & LIMB_MASK


def take_first(first, second):
    r1a, r0a, n1a, n0a, clear_a, ord_a = first
    r1b, r0b, n1b, n0b, clear_b, ord_b = second
    low = n0a * r0b - n0b * r0a + ((ord_b - ord_a) >> 31)
    mid = (n1a * r0b + n0a * r1b) - (n1b * r0a + n0b * r1a) + (low >> LIMB_BITS)
    high = n1a * r1b - n1b * r1a + (mid >> LIMB_BITS)
    return high >= clear_b - clear_a


def pick(take, first, second):
    return tuple(jnp.where(take, one, two) for one, two in zip(first, second))


def joined(entry):
    r1, r0, n1, n0, clear, order = entry
    return (r1 << LIMB_BITS) | r0, (n1 << LIMB_BITS) | n0, clear, order


def split(value):
    high = value.astype(jnp.bfloat16)
    return high, (value - high.astype(jnp.float32)).astype(jnp.bfloat16)


def iota(shape, axis):
    return lax.broadcasted_iota(jnp.int32, shape, axis)


def row_weights(own):
    chunk = own // 2
    table = np.zeros((4, 16 * TILE, LANES))
    for core in range(2):
        for outer in range(2):
            def image(r):
                return np.eye(own)[r] if 0 <= r < own else np.zeros(own)

            def inside(level, row):
                count = own >> level
                beyond = row < 0 if core == 0 else row >= count
                return outer == 1 or not beyond

            def level_row(level, row):
                if level == 0:
                    return image(row)
                if not inside(level, row):
                    return np.zeros(own)
                return sum(TAPS[d] * level_row(level - 1, 2 * row - 2 + d) for d in range(6))

            rows = {}
            above = [[-1], [-2, -1], [-2, -1]]
            for level in range(1, LEVELS + 1):
                count = own >> level
                below = [[count], [count, count + 1], [count, count + 1]][level - 1]
                outside, beside = (above[level - 1], below) if core == 0 else (below, above[level - 1])
                first = 0 if level == 1 else 2
                for band in range(2):
                    for base, picked in ((0, outside), (TILE, beside)):
                        for n, row in enumerate(picked):
                            rows[level, base + first + band * len(picked) + n] = (band, level_row(level, row))
                    start = 2 * TILE + (2 if level == 3 else 0)
                    for n in range(count):
                        rows[level, start + band * count + n] = (band, level_row(level, n))
            for (level, m), (band, weights) in rows.items():
                for k in range(4 * own):
                    slot, within = k // (4 * chunk), k % chunk
                    if (k // chunk) % 2 != band:
                        continue
                    place = slot if core == 0 else 1 - slot
                    value = weights[place * chunk + within] * SCALE_BAND
                    top = np.float64(np.asarray(value, jnp.bfloat16))
                    table[2 * core + outer, (level - 1) * 4 * TILE + m, k] = top
                    if level == LEVELS:
                        table[2 * core + outer, level * 4 * TILE + m, k] = value - top
    return table.astype(jnp.bfloat16)


def kernel(
    red, nir, cloud, ordinals, table, out_red, out_nir, out_ord, out_1, out_2, out_3,
    stream, best, arrived, wide_0, wide_1, wide_2, message, received, weights,
    ords, load_sem, order_sem, send_sem, best_sem, sum_sem, pieces,
):
    tile = lax.axis_index("tiles")
    strip_index = lax.axis_index("rows")
    core = lax.axis_index("dates")
    strips = lax.axis_size("rows")
    dates, strip, width = red.shape
    chunk = strip // 4
    half = width // 2
    has_outer = jnp.where(core == 0, strip_index > 0, strip_index < strips - 1)
    outer_strip = jnp.clip(strip_index + 2 * core - 1, 0, strips - 1)
    partner = (tile, strip_index, 1 - core)
    outer = (tile, outer_strip, 1 - core)
    rows_of = [(3 - 3 * core) * chunk, (2 - core) * chunk, 3 * core * chunk, (1 + core) * chunk]

    arrivals = []
    for number, (slot, start, size) in enumerate(pieces):
        begin = pl.multiple_of(rows_of[slot], chunk)
        columns = pl.ds(start, size)
        for band, source in enumerate((red, nir, cloud)):
            pltpu.make_async_copy(
                source.at[:, pl.ds(begin, chunk), columns],
                stream.at[slot, band, :, :, columns],
                load_sem.at[number],
            ).start()
        whole = stream.at[slot, :, :, :, columns]
        arrivals.append(pltpu.make_async_copy(whole, whole, load_sem.at[number]))
    order_copy = pltpu.make_async_copy(ordinals, ords, order_sem.at[0])
    order_copy.start()
    case = 2 * core + has_outer.astype(jnp.int32)
    table_copy = pltpu.make_async_copy(table.at[case], weights, order_sem.at[1])
    table_copy.start()

    barrier = pltpu.get_barrier_semaphore()
    pl.semaphore_signal(barrier, inc=1, device_id=partner, device_id_type=MESH)

    @pl.when(has_outer)
    def _():
        pl.semaphore_signal(barrier, inc=1, device_id=outer, device_id_type=MESH)

    k = iota((4 * LANES, LANES), 0)
    j = iota((4 * LANES, LANES), 1)
    column_weights = taps(k - LANES - (2 * j - 2)).astype(jnp.bfloat16)

    @pl.when(jnp.logical_not(has_outer))
    def _():
        received[0] = jnp.zeros(received.shape[1:], jnp.float32)

    for wide in (wide_0, wide_1, wide_2):
        edge = jnp.zeros((wide.shape[0], LANES), jnp.bfloat16)
        wide[:, 0:LANES] = edge
        wide[:, wide.shape[1] - LANES :] = edge

    order_copy.wait()

    def find_best(slot, start, size, own):
        place = slot - 2

        def step(number, unused):
            at = pl.multiple_of(number * WIDTH + start, WIDTH)
            columns = pl.ds(at, WIDTH)

            def entry(date):
                red_hi, red_lo = limbs(stream[slot, 0, date, :, columns])
                nir_hi, nir_lo = limbs(stream[slot, 1, date, :, columns])
                clear = jnp.where(stream[slot, 2, date, :, columns] == 0, FLAG, 0)
                return (red_hi, red_lo, nir_hi, nir_lo, clear, ords[date])

            current = None
            if own:
                red_hi, red_lo = limbs(arrived[place, 0, :, columns])
                nir_hi, nir_lo = limbs(arrived[place, 1, :, columns])
                packed = arrived[place, 2, :, columns]
                current = (red_hi, red_lo, nir_hi, nir_lo, packed & FLAG, packed & (FLAG - 1))
            for date in range(0, dates, 2):
                other = entry(date)
                if date + 1 < dates:
                    later = entry(date + 1)
                    other = pick(take_first(later, other), later, other)
                current = other if current is None else pick(take_first(other, current), other, current)
            value_red, value_nir, clear, order = joined(current)
            if own:
                out_row = (core if place == 0 else 1 - core) * chunk
                rows = pl.ds(pl.multiple_of(out_row, chunk), chunk)
                out_red[rows, columns] = value_red
                out_nir[rows, columns] = value_nir
                out_ord[rows, columns] = order
                inner = pl.ds(pl.multiple_of(at + LANES, LANES), WIDTH)
                both = jnp.concatenate([value_red, value_nir], axis=0).astype(jnp.float32)
                high, low = split(both)
                base = place * 4 * chunk
                wide_0[base : base + 2 * chunk, inner] = high
                wide_0[base + 2 * chunk : base + 4 * chunk, inner] = low
            else:
                best[slot, 0, :, columns] = value_red
                best[slot, 1, :, columns] = value_nir
                best[slot, 2, :, columns] = clear + order
            return unused

        lax.fori_loop(0, size // WIDTH, step, 0)

    def best_copy(slot, part):
        columns = pl.ds(part * half, half)
        return pltpu.make_async_remote_copy(
            src_ref=best.at[slot, :, :, columns],
            dst_ref=arrived.at[slot, :, :, columns],
            send_sem=send_sem.at[0],
            recv_sem=best_sem.at[slot, part],
            device_id=partner,
            device_id_type=MESH,
        )

    waiting = list(zip(pieces, arrivals))

    def run(slot, part):
        begin, end = part * half, (part + 1) * half
        at = begin
        while at < end:
            if waiting and waiting[0][0][:2] == (slot, at):
                waiting.pop(0)[1].wait()
            stop = min([end] + [piece[1] for piece, _ in waiting if piece[0] == slot and piece[1] > at])
            find_best(slot, at, stop - at, slot >= 2)
            at = stop

    for slot in range(2):
        for part in range(2):
            run(slot, part)
            if slot == 0 and part == 0:
                pl.semaphore_wait(barrier, 1 + has_outer.astype(jnp.int32))
            best_copy(slot, part).start()
    for slot in range(2):
        for part in range(2):
            best_copy(slot, part).wait_recv()
            run(slot + 2, part)
    table_copy.wait()

    def filter_columns(source):
        blocks = (source.shape[1] - 2 * LANES) // (2 * LANES)
        left = jnp.concatenate([source[:, 2 * LANES * b : 2 * LANES * b + 4 * LANES] for b in range(blocks)], axis=0)
        out = jnp.dot(left, column_weights, preferred_element_type=jnp.float32)
        count = source.shape[0]
        group = 2 * chunk
        places = []
        for place in range(2):
            parts = []
            for b in range(blocks):
                row = b * count + place * 2 * group
                parts.append(out[row : row + group] + out[row + group : row + 2 * group])
            places.append(split(jnp.concatenate(parts, axis=1)))
        return jnp.concatenate([value for pair in places for value in pair], axis=0)

    def filter_rows(level, data, count):
        left = weights[(level - 1) * 4 * TILE : ((level - 1) * 4 + count) * TILE, 0 : data.shape[0]]
        return jnp.dot(left, data, preferred_element_type=jnp.float32)

    data_1 = filter_columns(wide_0)
    wide_1[:, LANES : LANES + half] = data_1
    data_2 = filter_columns(wide_1)
    wide_2[:, LANES : LANES + half // 2] = data_2
    data_3 = filter_columns(wide_2)
    level_1 = filter_rows(1, data_1, 4)
    level_2 = filter_rows(2, data_2, 4)
    level_3 = filter_rows(3, data_3, 8)
    level_3 = level_3[0 : 3 * TILE] + level_3[4 * TILE : 7 * TILE]
    ends = (half // 2, half // 2 + half // 4)

    def sums(side):
        rows = slice(side * TILE, (side + 1) * TILE)
        one, two, three = level_1[rows], level_2[rows], level_3[rows]
        message[side, :, 0 : ends[0]] = one[:, 0 : ends[0]] + two
        message[side, :, ends[0] : ends[1]] = one[:, ends[0] : ends[1]] + three
        message[side, :, ends[1] :] = one[:, ends[1] :]

    def sum_copy(side, device):
        return pltpu.make_async_remote_copy(
            src_ref=message.at[side],
            dst_ref=received.at[side],
            send_sem=send_sem.at[1 + side],
            recv_sem=sum_sem.at[side],
            device_id=device,
            device_id_type=MESH,
        )

    to_outer, to_partner = sum_copy(0, outer), sum_copy(1, partner)
    sums(0)

    @pl.when(has_outer)
    def _():
        to_outer.start()

    sums(1)
    to_partner.start()
    to_partner.wait_recv()

    @pl.when(has_outer)
    def _():
        to_outer.wait_recv()

    def spread(side, row, columns):
        return jnp.broadcast_to(received[side, row : row + 1, columns], (TILE, columns.stop - columns.start))

    row = iota((TILE, half), 0)
    edges = ((TILE - 1) * core, (TILE - 1) * (1 - core))
    for band in range(2):
        total = level_1[(2 + band) * TILE : (3 + band) * TILE]
        for side in range(2):
            total = total + jnp.where(row == edges[side], spread(side, band, slice(0, half)), 0.0)
        out_1[band] = total
    row = iota((TILE, ends[0]), 0)
    total = level_2[2 * TILE : 3 * TILE]
    for side in range(2):
        shift = 2 * (core if side == 0 else 1 - core)
        for number in range(4):
            target = number % 2 + 4 * (number // 2) + shift
            total = total + jnp.where(row == target, spread(side, 2 + number, slice(0, ends[0])), 0.0)
    out_2[0] = total[0:4]
    out_2[1] = total[4:8]
    total = level_3[2 * TILE : 3 * TILE] + received[0, :, ends[0] : ends[1]] + received[1, :, ends[0] : ends[1]]
    out_3[0] = total[2:4]
    out_3[1] = total[4:6]

    pltpu.make_async_copy(best, best, send_sem.at[0]).wait()
    to_partner.wait_send()

    @pl.when(has_outer)
    def _():
        to_outer.wait_send()


def write_out(*refs):
    count = len(refs) // 2
    semaphores = refs[-1]
    copies = [pltpu.make_async_copy(refs[n], refs[count + n], semaphores.at[n]) for n in range(count)]
    for copy in copies:
        copy.start()
    for copy in copies:
        copy.wait()


def body(red_band, nir_band, cloud_class, date_ordinal):
    dates, strip, width = red_band.shape
    own = strip // 2
    chunk = strip // 4
    half = width // 2
    whole = pl.BlockSpec(memory_space=pltpu.VMEM)
    anywhere = pl.BlockSpec(memory_space=pl.ANY)
    outs = [jax.ShapeDtypeStruct((own, width), jnp.int32)] * 3
    outs += [jax.ShapeDtypeStruct((2, own >> n, width >> n), jnp.float32) for n in range(1, LEVELS + 1)]
    kept = [pltpu.VMEM(out.shape, out.dtype) for out in outs]
    pieces = [(0, 0, half // 2), (0, half // 2, half // 2), (0, half, half)] + [(slot, 0, width) for slot in range(1, 4)]
    pieces = tuple(pieces)
    table = row_weights(own)

    def run(*refs):
        kernel(*refs, pieces=pieces)

    results = pl.pallas_call(
        run,
        out_shape=kept,
        in_specs=[anywhere] * 5,
        out_specs=[whole] * 6,
        scratch_shapes=[
            pltpu.VMEM((4, 3, dates, chunk, width), jnp.int32),
            pltpu.VMEM((2, 3, chunk, width), jnp.int32),
            pltpu.VMEM((2, 3, chunk, width), jnp.int32),
            pltpu.VMEM((8 * chunk, width + 2 * LANES), jnp.bfloat16),
            pltpu.VMEM((8 * chunk, width // 2 + 2 * LANES), jnp.bfloat16),
            pltpu.VMEM((8 * chunk, width // 4 + 2 * LANES), jnp.bfloat16),
            pltpu.VMEM((2, TILE, half), jnp.float32),
            pltpu.VMEM((2, TILE, half), jnp.float32),
            pltpu.VMEM(table.shape[1:], jnp.bfloat16),
            pltpu.SMEM((dates,), jnp.int32),
            pltpu.SemaphoreType.DMA((len(pieces),)),
            pltpu.SemaphoreType.DMA((2,)),
            pltpu.SemaphoreType.DMA((3,)),
            pltpu.SemaphoreType.DMA((2, 2)),
            pltpu.SemaphoreType.DMA((2,)),
        ],
        compiler_params=pltpu.CompilerParams(collective_id=0, has_side_effects=True),
        name="composite",
    )(red_band, nir_band, cloud_class, date_ordinal, jnp.asarray(table))
    return pl.pallas_call(
        write_out,
        out_shape=outs,
        in_specs=[whole] * 6,
        out_specs=[anywhere] * 6,
        scratch_shapes=[pltpu.SemaphoreType.DMA((6,))],
        name="write_out",
    )(*[pltpu.with_memory_space_constraint(result, pltpu.VMEM) for result in results])


def solution(mesh):
    in_specs = (
        P("dates", ("tiles", "rows"), None),
        P("dates", ("tiles", "rows"), None),
        P("dates", ("tiles", "rows"), None),
        P(("tiles", "dates")),
    )
    out_specs = (
        P(("tiles", "rows", "dates"), None),
        P(("tiles", "rows", "dates"), None),
        P(("tiles", "rows", "dates"), None),
        P(None, ("tiles", "rows", "dates"), None),
        P(None, ("tiles", "rows", "dates"), None),
        P(None, ("tiles", "rows", "dates"), None),
    )
    return jax.shard_map(body, mesh=mesh, in_specs=in_specs, out_specs=out_specs, check_vma=False)
```

time: 12.8 us -> 12.2 us (0.953)
  the two profiles are of different devices: /device:TPU:0 before, /device:TPU:1 now
where the time goes in v1:
time: 12.2 us; the launch traced here: 12.1 us
  Pallas kernels  11.4 us (93%)
  between operations  0.64 us (5%)
    pallas_call x1, Pallas kernels, body(): pl.pallas_call(run, out_shape=kept, in_specs=[anywhere] * 5, out_specs=[w...  10.6 us
    pallas_call x1, Pallas kernels, body(): pl.pallas_call(write_out, out_shape=outs, in_specs=[whole] * 6, out_specs...  0.82 us

profile of v1, /device:TPU:1, one launch (start us, length us, event | category | flops | bytes accessed | tf_op | source)
XLA Modules:
  0.0 12.1 jit_solution(5025612337884447134)
XLA Ops:
  0.6 10.6 %composite.1 = (s32[16,2048]{1,0:T(8,128)S(1)}, s32[16,2048]{1,0:T(8,128)S(1)}, s32[16,2048]{1,0:T(8,128)S(1)}, f32[2,8,1024]{2,1,0:T(8,128)S(1)}, f32[2,4,512]{2,1,0:T(4,128)S(1)}, /*index=5*/f32[2,2,256]{2,1,0:T(2,128)S(1)}) custom-call(s32[12,32,2048]{2,1,0:T(8,128)} %refs_0_.1, s32[12,32,2048]{2,1,0:T(8,128)} %refs_1_.1, s32[12,32,2048]{2,1,0:T(8,128)} %refs_2_.1, ...), custom_call_target="tpu_custom_call" | custom-call | tf_op jit(solution)/shard_map/composite/pallas_call | solution.py:366
  11.3 0.8 %write_out.1 = (s32[16,2048]{1,0:T(8,128)}, s32[16,2048]{1,0:T(8,128)}, s32[16,2048]{1,0:T(8,128)}, f32[2,8,1024]{2,1,0:T(8,128)}, f32[2,4,512]{2,1,0:T(4,128)}, /*index=5*/f32[2,2,256]{2,1,0:T(2,128)}) custom-call(s32[16,2048]{1,0:T(8,128)S(1)} %get-tuple-element.12.refs_0_, s32[16,2048]{1,0:T(8,128)S(1)} %get-tuple-element.13.refs_1_, ...), custom_call_target="tpu_custom_call" | custom-call | tf_op jit(solution)/shard_map/write_out/pallas_call | solution.py:391

commit v2 on v1

--- a/solution.py
+++ b/solution.py
@@ -106,7 +106,7 @@
 
 def kernel(
     red, nir, cloud, ordinals, table, out_red, out_nir, out_ord, out_1, out_2, out_3,
-    stream, best, arrived, wide_0, wide_1, wide_2, message, received, weights,
+    stream, best, arrived, merged, wide_0, wide_1, wide_2, message, received, home, homed, weights,
     ords, load_sem, order_sem, send_sem, best_sem, sum_sem, pieces,
 ):
     tile = lax.axis_index("tiles")
@@ -116,11 +116,13 @@
     dates, strip, width = red.shape
     chunk = strip // 4
     half = width // 2
-    has_outer = jnp.where(core == 0, strip_index > 0, strip_index < strips - 1)
-    outer_strip = jnp.clip(strip_index + 2 * core - 1, 0, strips - 1)
+    toward = 1 - 2 * core
+    has_target = jnp.where(core == 0, strip_index < strips - 1, strip_index > 0)
+    has_source = jnp.where(core == 0, strip_index > 0, strip_index < strips - 1)
     partner = (tile, strip_index, 1 - core)
-    outer = (tile, outer_strip, 1 - core)
-    rows_of = [(3 - 3 * core) * chunk, (2 - core) * chunk, 3 * core * chunk, (1 + core) * chunk]
+    target = (tile, jnp.clip(strip_index + toward, 0, strips - 1), core)
+    source_device = (tile, jnp.clip(strip_index - toward, 0, strips - 1), core)
+    rows_of = [3 * core * chunk, (1 + core) * chunk, (3 - 3 * core) * chunk, (2 - core) * chunk]
 
     arrivals = []
     for number, (slot, start, size) in enumerate(pieces):
@@ -136,24 +138,24 @@
         arrivals.append(pltpu.make_async_copy(whole, whole, load_sem.at[number]))
     order_copy = pltpu.make_async_copy(ordinals, ords, order_sem.at[0])
     order_copy.start()
-    case = 2 * core + has_outer.astype(jnp.int32)
+    case = 2 * (1 - core) + has_target.astype(jnp.int32)
     table_copy = pltpu.make_async_copy(table.at[case], weights, order_sem.at[1])
     table_copy.start()
 
     barrier = pltpu.get_barrier_semaphore()
     pl.semaphore_signal(barrier, inc=1, device_id=partner, device_id_type=MESH)
 
-    @pl.when(has_outer)
+    @pl.when(has_source)
     def _():
-        pl.semaphore_signal(barrier, inc=1, device_id=outer, device_id_type=MESH)
+        pl.semaphore_signal(barrier, inc=1, device_id=source_device, device_id_type=MESH)
 
     k = iota((4 * LANES, LANES), 0)
     j = iota((4 * LANES, LANES), 1)
     column_weights = taps(k - LANES - (2 * j - 2)).astype(jnp.bfloat16)
 
-    @pl.when(jnp.logical_not(has_outer))
+    @pl.when(jnp.logical_not(has_source))
     def _():
-        received[0] = jnp.zeros(received.shape[1:], jnp.float32)
+        received[...] = jnp.zeros(received.shape, jnp.float32)
 
     for wide in (wide_0, wide_1, wide_2):
         edge = jnp.zeros((wide.shape[0], LANES), jnp.bfloat16)
@@ -189,11 +191,9 @@
                 current = other if current is None else pick(take_first(other, current), other, current)
             value_red, value_nir, clear, order = joined(current)
             if own:
-                out_row = (core if place == 0 else 1 - core) * chunk
-                rows = pl.ds(pl.multiple_of(out_row, chunk), chunk)
-                out_red[rows, columns] = value_red
-                out_nir[rows, columns] = value_nir
-                out_ord[rows, columns] = order
+                merged[place, 0, :, columns] = value_red
+                merged[place, 1, :, columns] = value_nir
+                merged[place, 2, :, columns] = order
                 inner = pl.ds(pl.multiple_of(at + LANES, LANES), WIDTH)
                 both = jnp.concatenate([value_red, value_nir], axis=0).astype(jnp.float32)
                 high, low = split(both)
@@ -235,12 +235,22 @@
         for part in range(2):
             run(slot, part)
             if slot == 0 and part == 0:
-                pl.semaphore_wait(barrier, 1 + has_outer.astype(jnp.int32))
+                pl.semaphore_wait(barrier, 1 + has_target.astype(jnp.int32))
             best_copy(slot, part).start()
     for slot in range(2):
         for part in range(2):
             best_copy(slot, part).wait_recv()
             run(slot + 2, part)
+        merged_rows = pl.ds(pl.multiple_of(((1 - core) if slot == 0 else core) * chunk, chunk), chunk)
+        for number, result in enumerate((out_red, out_nir, out_ord)):
+            pltpu.make_async_remote_copy(
+                src_ref=merged.at[slot, number],
+                dst_ref=result.at[merged_rows],
+                send_sem=send_sem.at[1],
+                recv_sem=sum_sem.at[0],
+                device_id=partner,
+                device_id_type=MESH,
+            ).start()
     table_copy.wait()
 
     def filter_columns(source):
@@ -273,50 +283,62 @@
     level_3 = level_3[0 : 3 * TILE] + level_3[4 * TILE : 7 * TILE]
     ends = (half // 2, half // 2 + half // 4)
 
-    def sums(side):
+    def sums(side, held):
         rows = slice(side * TILE, (side + 1) * TILE)
         one, two, three = level_1[rows], level_2[rows], level_3[rows]
-        message[side, :, 0 : ends[0]] = one[:, 0 : ends[0]] + two
-        message[side, :, ends[0] : ends[1]] = one[:, ends[0] : ends[1]] + three
-        message[side, :, ends[1] :] = one[:, ends[1] :]
-
-    def sum_copy(side, device):
-        return pltpu.make_async_remote_copy(
-            src_ref=message.at[side],
-            dst_ref=received.at[side],
-            send_sem=send_sem.at[1 + side],
-            recv_sem=sum_sem.at[side],
-            device_id=device,
-            device_id_type=MESH,
-        )
-
-    to_outer, to_partner = sum_copy(0, outer), sum_copy(1, partner)
-    sums(0)
-
-    @pl.when(has_outer)
+        held[:, 0 : ends[0]] = one[:, 0 : ends[0]] + two
+        held[:, ends[0] : ends[1]] = one[:, ends[0] : ends[1]] + three
+        held[:, ends[1] :] = one[:, ends[1] :]
+
+    to_target = pltpu.make_async_remote_copy(
+        src_ref=message.at[0],
+        dst_ref=received,
+        send_sem=send_sem.at[2],
+        recv_sem=sum_sem.at[1],
+        device_id=target,
+        device_id_type=MESH,
+    )
+    to_partner = pltpu.make_async_remote_copy(
+        src_ref=home,
+        dst_ref=homed,
+        send_sem=send_sem.at[3],
+        recv_sem=sum_sem.at[2],
+        device_id=partner,
+        device_id_type=MESH,
+    )
+    sums(0, message.at[0])
+
+    @pl.when(has_target)
     def _():
-        to_outer.start()
-
-    sums(1)
+        to_target.start()
+
+    home[0 : 2 * TILE] = level_1[2 * TILE : 4 * TILE]
+    home[2 * TILE :, 0 : ends[0]] = level_2[2 * TILE : 3 * TILE]
+    home[2 * TILE :, ends[0] : ends[1]] = level_3[2 * TILE : 3 * TILE]
+    home[2 * TILE :, ends[1] :] = jnp.zeros((TILE, half - ends[1]), jnp.float32)
     to_partner.start()
+    sums(1, message.at[1])
     to_partner.wait_recv()
-
-    @pl.when(has_outer)
+    pltpu.make_async_copy(merged, merged, sum_sem.at[0]).wait()
+
+    @pl.when(has_source)
     def _():
-        to_outer.wait_recv()
+        to_target.wait_recv()
+
+    sides = (received, message.at[1])
 
     def spread(side, row, columns):
-        return jnp.broadcast_to(received[side, row : row + 1, columns], (TILE, columns.stop - columns.start))
+        return jnp.broadcast_to(sides[side][row : row + 1, columns], (TILE, columns.stop - columns.start))
 
     row = iota((TILE, half), 0)
     edges = ((TILE - 1) * core, (TILE - 1) * (1 - core))
     for band in range(2):
-        total = level_1[(2 + band) * TILE : (3 + band) * TILE]
+        total = homed[band * TILE : (band + 1) * TILE]
         for side in range(2):
             total = total + jnp.where(row == edges[side], spread(side, band, slice(0, half)), 0.0)
         out_1[band] = total
     row = iota((TILE, ends[0]), 0)
-    total = level_2[2 * TILE : 3 * TILE]
+    total = homed[2 * TILE :, 0 : ends[0]]
     for side in range(2):
         shift = 2 * (core if side == 0 else 1 - core)
         for number in range(4):
@@ -324,16 +346,18 @@
             total = total + jnp.where(row == target, spread(side, 2 + number, slice(0, ends[0])), 0.0)
     out_2[0] = total[0:4]
     out_2[1] = total[4:8]
-    total = level_3[2 * TILE : 3 * TILE] + received[0, :, ends[0] : ends[1]] + received[1, :, ends[0] : ends[1]]
+    third = slice(ends[0], ends[1])
+    total = homed[2 * TILE :, third] + sides[0][:, third] + sides[1][:, third]
     out_3[0] = total[2:4]
     out_3[1] = total[4:6]
 
     pltpu.make_async_copy(best, best, send_sem.at[0]).wait()
+    pltpu.make_async_copy(merged, merged, send_sem.at[1]).wait()
     to_partner.wait_send()
 
-    @pl.when(has_outer)
+    @pl.when(has_target)
     def _():
-        to_outer.wait_send()
+        to_target.wait_send()
 
 
 def write_out(*refs):
@@ -356,8 +380,8 @@
     outs = [jax.ShapeDtypeStruct((own, width), jnp.int32)] * 3
     outs += [jax.ShapeDtypeStruct((2, own >> n, width >> n), jnp.float32) for n in range(1, LEVELS + 1)]
     kept = [pltpu.VMEM(out.shape, out.dtype) for out in outs]
-    pieces = [(0, 0, half // 2), (0, half // 2, half // 2), (0, half, half)] + [(slot, 0, width) for slot in range(1, 4)]
-    pieces = tuple(pieces)
+    pieces = [(0, start, half // 2) for start in range(0, width, half // 2)]
+    pieces += [(slot, start, half) for slot in range(1, 4) for start in (0, half)]
     table = row_weights(own)
 
     def run(*refs):
@@ -372,18 +396,21 @@
             pltpu.VMEM((4, 3, dates, chunk, width), jnp.int32),
             pltpu.VMEM((2, 3, chunk, width), jnp.int32),
             pltpu.VMEM((2, 3, chunk, width), jnp.int32),
+            pltpu.VMEM((2, 3, chunk, width), jnp.int32),
             pltpu.VMEM((8 * chunk, width + 2 * LANES), jnp.bfloat16),
             pltpu.VMEM((8 * chunk, width // 2 + 2 * LANES), jnp.bfloat16),
             pltpu.VMEM((8 * chunk, width // 4 + 2 * LANES), jnp.bfloat16),
             pltpu.VMEM((2, TILE, half), jnp.float32),
-            pltpu.VMEM((2, TILE, half), jnp.float32),
+            pltpu.VMEM((TILE, half), jnp.float32),
+            pltpu.VMEM((3 * TILE, half), jnp.float32),
+            pltpu.VMEM((3 * TILE, half), jnp.float32),
             pltpu.VMEM(table.shape[1:], jnp.bfloat16),
             pltpu.SMEM((dates,), jnp.int32),
             pltpu.SemaphoreType.DMA((len(pieces),)),
             pltpu.SemaphoreType.DMA((2,)),
+            pltpu.SemaphoreType.DMA((4,)),
+            pltpu.SemaphoreType.DMA((2, 2)),
             pltpu.SemaphoreType.DMA((3,)),
-            pltpu.SemaphoreType.DMA((2, 2)),
-            pltpu.SemaphoreType.DMA((2,)),
         ],
         compiler_params=pltpu.CompilerParams(collective_id=0, has_side_effects=True),
         name="composite",

time: 12.2 us -> 11.2 us (0.918)
  Pallas kernels: 11.4 us -> 10.4 us
    pallas_call x1, Pallas kernels: 10.6 us -> 9.6 us  [body(): pl.pallas_call(run, out_shape=kept, in_specs=[anywhere] * 5, out_specs=[w...]
where the time goes in v2:
time: 11.2 us; the launch traced here: 11.1 us
  Pallas kernels  10.4 us (93%)
  between operations  0.64 us (6%)
    pallas_call x1, Pallas kernels, body(): pl.pallas_call(run, out_shape=kept, in_specs=[anywhere] * 5, out_specs=[w...  9.6 us
    pallas_call x1, Pallas kernels, body(): pl.pallas_call(write_out, out_shape=outs, in_specs=[whole] * 6, out_specs...  0.82 us

profile of v2, /device:TPU:1, one launch (start us, length us, event | category | flops | bytes accessed | tf_op | source)
XLA Modules:
  0.0 11.1 jit_solution(17332168642256299516)
XLA Ops:
  0.6 9.6 %composite.1 = (s32[16,2048]{1,0:T(8,128)S(1)}, s32[16,2048]{1,0:T(8,128)S(1)}, s32[16,2048]{1,0:T(8,128)S(1)}, f32[2,8,1024]{2,1,0:T(8,128)S(1)}, f32[2,4,512]{2,1,0:T(4,128)S(1)}, /*index=5*/f32[2,2,256]{2,1,0:T(2,128)S(1)}) custom-call(s32[12,32,2048]{2,1,0:T(8,128)} %refs_0_.1, s32[12,32,2048]{2,1,0:T(8,128)} %refs_1_.1, s32[12,32,2048]{2,1,0:T(8,128)} %refs_2_.1, ...), custom_call_target="tpu_custom_call" | custom-call | tf_op jit(solution)/shard_map/composite/pallas_call | solution.py:390
  10.2 0.8 %write_out.1 = (s32[16,2048]{1,0:T(8,128)}, s32[16,2048]{1,0:T(8,128)}, s32[16,2048]{1,0:T(8,128)}, f32[2,8,1024]{2,1,0:T(8,128)}, f32[2,4,512]{2,1,0:T(4,128)}, /*index=5*/f32[2,2,256]{2,1,0:T(2,128)}) custom-call(s32[16,2048]{1,0:T(8,128)S(1)} %get-tuple-element.12.refs_0_, s32[16,2048]{1,0:T(8,128)S(1)} %get-tuple-element.13.refs_1_, ...), custom_call_target="tpu_custom_call" | custom-call | tf_op jit(solution)/shard_map/write_out/pallas_call | solution.py:418

commit v3 on v2

--- a/solution.py
+++ b/solution.py
@@ -14,15 +14,13 @@
 LANES = 128
 TILE = 8
 WIDTH = 512
+AT_2, AT_3 = 3, 71
 MESH = pl.DeviceIdType.MESH
 TAPS = np.array([1, 5, 10, 10, 5, 1], np.float64) / 32
 
 
-def taps(distance):
-    far = (distance == 0) | (distance == 5)
-    mid = (distance == 1) | (distance == 4)
-    near = (distance == 2) | (distance == 3)
-    return jnp.where(near, 0.3125, jnp.where(mid, 0.15625, jnp.where(far, 0.03125, 0.0)))
+def tap(distance):
+    return TAPS[distance] if 0 <= distance < len(TAPS) else 0.0
 
 
 def limbs(value):
@@ -56,57 +54,78 @@
     return lax.broadcasted_iota(jnp.int32, shape, axis)
 
 
+def column_weights():
+    columns = range(2 * LANES)
+    one = {j: np.array([tap(c - 2 * j + 2) for c in columns]) for j in range(-12, LANES + 12)}
+    two = {i: sum(TAPS[d] * one[2 * i - 2 + d] for d in range(6)) for i in range(-5, LANES // 2 + 5)}
+    three = {p: sum(TAPS[d] * two[2 * p - 2 + d] for d in range(6)) for p in range(-1, LANES // 4 + 1)}
+    three[-2] = sum(TAPS[d] * two[-6 + d] for d in range(1, 6))
+    three[LANES // 4 + 1] = sum(TAPS[d] * two[LANES // 2 + d] for d in range(5))
+    table = np.zeros((2 * LANES, 3 * LANES))
+    for j in range(LANES):
+        table[:, j] = one[j]
+    table[:, LANES] = one[LANES]
+    table[:, 2 * LANES - 1] = one[-1]
+    for i in range(-2, LANES // 2 + 2):
+        table[:, LANES + AT_2 + i] = two[i]
+    for p in range(-2, LANES // 4 + 2):
+        top = three[p].astype(jnp.bfloat16).astype(np.float64)
+        table[:, LANES + AT_3 + p] = top
+        table[:, 2 * LANES + AT_3 + p] = three[p] - top
+    return table.astype(jnp.bfloat16)
+
+
 def row_weights(own):
     chunk = own // 2
-    table = np.zeros((4, 16 * TILE, LANES))
-    for core in range(2):
+    table = np.zeros((4, 8 * TILE, LANES))
+    for side in range(2):
         for outer in range(2):
-            def image(r):
-                return np.eye(own)[r] if 0 <= r < own else np.zeros(own)
-
-            def inside(level, row):
-                count = own >> level
-                beyond = row < 0 if core == 0 else row >= count
-                return outer == 1 or not beyond
 
             def level_row(level, row):
                 if level == 0:
-                    return image(row)
-                if not inside(level, row):
+                    return np.eye(own)[row] if 0 <= row < own else np.zeros(own)
+                beyond = row < 0 if side == 0 else row >= own >> level
+                if beyond and not outer:
                     return np.zeros(own)
                 return sum(TAPS[d] * level_row(level - 1, 2 * row - 2 + d) for d in range(6))
 
-            rows = {}
-            above = [[-1], [-2, -1], [-2, -1]]
-            for level in range(1, LEVELS + 1):
-                count = own >> level
-                below = [[count], [count, count + 1], [count, count + 1]][level - 1]
-                outside, beside = (above[level - 1], below) if core == 0 else (below, above[level - 1])
-                first = 0 if level == 1 else 2
-                for band in range(2):
-                    for base, picked in ((0, outside), (TILE, beside)):
-                        for n, row in enumerate(picked):
-                            rows[level, base + first + band * len(picked) + n] = (band, level_row(level, row))
-                    start = 2 * TILE + (2 if level == 3 else 0)
-                    for n in range(count):
-                        rows[level, start + band * count + n] = (band, level_row(level, n))
-            for (level, m), (band, weights) in rows.items():
+            def put(m, band, level, row, second=None):
+                weights = level_row(level, row) * SCALE_BAND
                 for k in range(4 * own):
-                    slot, within = k // (4 * chunk), k % chunk
                     if (k // chunk) % 2 != band:
                         continue
-                    place = slot if core == 0 else 1 - slot
-                    value = weights[place * chunk + within] * SCALE_BAND
+                    place = (k // own) % 2
+                    place = place if side == 0 else 1 - place
+                    value = weights[place * chunk + k % chunk]
                     top = np.float64(np.asarray(value, jnp.bfloat16))
-                    table[2 * core + outer, (level - 1) * 4 * TILE + m, k] = top
-                    if level == LEVELS:
-                        table[2 * core + outer, level * 4 * TILE + m, k] = value - top
+                    table[2 * side + outer, m, k] = top
+                    if second is not None:
+                        table[2 * side + outer, second, k] = value - top
+
+            for band in range(2):
+                for beside in range(2):
+                    ends = [(-1,), (-2, -1), (-2, -1)]
+                    low = (beside == 0) == (side == 0)
+                    rows = [[row if low else (own >> level + 1) - 1 - row for row in ends[level]] for level in range(LEVELS)]
+                    rows = [sorted(some) for some in rows]
+                    put(beside * TILE + 4 + band, band, 1, rows[0][0])
+                    for n in range(2):
+                        put(beside * TILE + 2 * band + n, band, 2, rows[1][n])
+                        m = 4 * beside + 2 * band + n
+                        put(2 * TILE + m, band, 3, rows[2][n], 7 * TILE + m)
+                for row in range(own // 4):
+                    put(3 * TILE + band * (own // 4) + row, band, 2, row)
+                for row in range(own // 2):
+                    put(4 * TILE + band * (own // 2) + row, band, 1, row)
+                for row in range(own // 8):
+                    m = band * (own // 8) + row
+                    put(6 * TILE + m, band, 3, row, 6 * TILE + 4 + m)
     return table.astype(jnp.bfloat16)
 
 
 def kernel(
-    red, nir, cloud, ordinals, table, out_red, out_nir, out_ord, out_1, out_2, out_3,
-    stream, best, arrived, merged, wide_0, wide_1, wide_2, message, received, home, homed, weights,
+    red, nir, cloud, ordinals, row_table, column_table, out_red, out_nir, out_ord, out_1, out_2, out_3,
+    stream, best, arrived, merged, parts, message, received, home, homed, third, weights, columns_by,
     ords, load_sem, order_sem, send_sem, best_sem, sum_sem, pieces,
 ):
     tile = lax.axis_index("tiles")
@@ -139,8 +158,12 @@
     order_copy = pltpu.make_async_copy(ordinals, ords, order_sem.at[0])
     order_copy.start()
     case = 2 * (1 - core) + has_target.astype(jnp.int32)
-    table_copy = pltpu.make_async_copy(table.at[case], weights, order_sem.at[1])
-    table_copy.start()
+    table_copies = [
+        pltpu.make_async_copy(row_table.at[case], weights, order_sem.at[1]),
+        pltpu.make_async_copy(column_table, columns_by, order_sem.at[2]),
+    ]
+    for copy in table_copies:
+        copy.start()
 
     barrier = pltpu.get_barrier_semaphore()
     pl.semaphore_signal(barrier, inc=1, device_id=partner, device_id_type=MESH)
@@ -149,18 +172,9 @@
     def _():
         pl.semaphore_signal(barrier, inc=1, device_id=source_device, device_id_type=MESH)
 
-    k = iota((4 * LANES, LANES), 0)
-    j = iota((4 * LANES, LANES), 1)
-    column_weights = taps(k - LANES - (2 * j - 2)).astype(jnp.bfloat16)
-
     @pl.when(jnp.logical_not(has_source))
     def _():
         received[...] = jnp.zeros(received.shape, jnp.float32)
-
-    for wide in (wide_0, wide_1, wide_2):
-        edge = jnp.zeros((wide.shape[0], LANES), jnp.bfloat16)
-        wide[:, 0:LANES] = edge
-        wide[:, wide.shape[1] - LANES :] = edge
 
     order_copy.wait()
 
@@ -194,12 +208,10 @@
                 merged[place, 0, :, columns] = value_red
                 merged[place, 1, :, columns] = value_nir
                 merged[place, 2, :, columns] = order
-                inner = pl.ds(pl.multiple_of(at + LANES, LANES), WIDTH)
                 both = jnp.concatenate([value_red, value_nir], axis=0).astype(jnp.float32)
                 high, low = split(both)
-                base = place * 4 * chunk
-                wide_0[base : base + 2 * chunk, inner] = high
-                wide_0[base + 2 * chunk : base + 4 * chunk, inner] = low
+                parts[0, place * 2 * chunk : (place + 1) * 2 * chunk, columns] = high
+                parts[1, place * 2 * chunk : (place + 1) * 2 * chunk, columns] = low
             else:
                 best[slot, 0, :, columns] = value_red
                 best[slot, 1, :, columns] = value_nir
@@ -251,45 +263,101 @@
                 device_id=partner,
                 device_id_type=MESH,
             ).start()
-    table_copy.wait()
-
-    def filter_columns(source):
-        blocks = (source.shape[1] - 2 * LANES) // (2 * LANES)
-        left = jnp.concatenate([source[:, 2 * LANES * b : 2 * LANES * b + 4 * LANES] for b in range(blocks)], axis=0)
-        out = jnp.dot(left, column_weights, preferred_element_type=jnp.float32)
-        count = source.shape[0]
-        group = 2 * chunk
-        places = []
-        for place in range(2):
-            parts = []
-            for b in range(blocks):
-                row = b * count + place * 2 * group
-                parts.append(out[row : row + group] + out[row + group : row + 2 * group])
-            places.append(split(jnp.concatenate(parts, axis=1)))
-        return jnp.concatenate([value for pair in places for value in pair], axis=0)
-
-    def filter_rows(level, data, count):
-        left = weights[(level - 1) * 4 * TILE : ((level - 1) * 4 + count) * TILE, 0 : data.shape[0]]
-        return jnp.dot(left, data, preferred_element_type=jnp.float32)
-
-    data_1 = filter_columns(wide_0)
-    wide_1[:, LANES : LANES + half] = data_1
-    data_2 = filter_columns(wide_1)
-    wide_2[:, LANES : LANES + half // 2] = data_2
-    data_3 = filter_columns(wide_2)
-    level_1 = filter_rows(1, data_1, 4)
-    level_2 = filter_rows(2, data_2, 4)
-    level_3 = filter_rows(3, data_3, 8)
-    level_3 = level_3[0 : 3 * TILE] + level_3[4 * TILE : 7 * TILE]
+    for copy in table_copies:
+        copy.wait()
+
+    block = 2 * LANES
+    blocks = width // block
+    count = 4 * chunk
+
+    def stacked(part):
+        return jnp.concatenate([parts[part, :, b * block : (b + 1) * block] for b in range(blocks)], axis=0)
+
+    def product(left, right):
+        return jnp.dot(left, right, preferred_element_type=jnp.float32)
+
+    high, low = stacked(0), stacked(1)
+    first = columns_by[:, 0:block]
+    shares = product(high, first) + product(low, first)
+    second = product(high, columns_by[:, block : block + LANES])
+    data = []
+    for b in range(blocks):
+        rows = slice(b * count, (b + 1) * count)
+        for value in (shares[rows, 0:LANES], shares[rows, LANES:] + second[rows]):
+            data.append(jnp.concatenate(split(value), axis=0))
+    sums = product(weights[:, 0 : 2 * count], jnp.concatenate(data, axis=1))
+    lane = iota((TILE, LANES), 1)
+
+    def tile_of(number, b, half_of):
+        at = b * block + half_of * LANES
+        return sums[number * TILE : (number + 1) * TILE, at : at + LANES]
+
+    def rolled(value, shift):
+        return pltpu.roll(value, shift % LANES, 1)
+
+    def only(mask, value):
+        return jnp.where(mask, value, 0.0)
+
+    def level_1(number):
+        tiles = []
+        for b in range(blocks):
+            value = tile_of(number, b, 0)
+            if b > 0:
+                value = value + only(lane == 0, tile_of(number, b - 1, 1))
+            if b + 1 < blocks:
+                value = value + only(lane == LANES - 1, tile_of(number, b + 1, 1))
+            tiles.append(value)
+        return tiles
+
+    def gathered(shares_of, at, per):
+        size = LANES // per
+        tiles = [None] * (blocks // per)
+
+        def put(number, value):
+            if 0 <= number < len(tiles):
+                tiles[number] = value if tiles[number] is None else tiles[number] + value
+
+        for b in range(blocks):
+            number, start = b // per, (b % per) * size
+            value = rolled(shares_of[b], start - at)
+            put(number, only((lane >= start - 2) & (lane < start + size + 2), value))
+            if b % per == 0:
+                put(number - 1, only(lane >= LANES - 2, value))
+            if b % per == per - 1:
+                put(number + 1, only(lane < 2, value))
+        return tiles
+
+    def level_2(number):
+        shares_of = [tile_of(number, b, 1) for b in range(blocks)]
+        tiles = gathered(shares_of, AT_2, 2)
+        left, right = shares_of[0], shares_of[-1]
+        tiles[0] = tiles[0] - only(lane == 0, rolled(left, 1) * TAPS[1])
+        tiles[-1] = tiles[-1] - only(lane == LANES - 1, rolled(right, -1) * TAPS[4])
+        return tiles
+
+    def level_3(shares_of):
+        tiles = gathered(shares_of, AT_3, 4)
+        left, right = shares_of[0], shares_of[-1]
+        edge = rolled(left, 2 - AT_2) * TAPS[0] + rolled(left, 1 - AT_2) * TAPS[1] + rolled(left, 1) * (TAPS[2] * TAPS[1])
+        next_edge = rolled(left, 2) * (TAPS[0] * TAPS[1])
+        tiles[0] = tiles[0] - only(lane == 0, edge) - only(lane == 1, next_edge)
+        beyond = AT_2 + LANES // 2
+        edge = rolled(right, -1 - beyond) * TAPS[4] + rolled(right, -2 - beyond) * TAPS[5]
+        edge = edge + rolled(right, -1) * (TAPS[3] * TAPS[4])
+        next_edge = rolled(right, -2) * (TAPS[5] * TAPS[4])
+        tiles[-1] = tiles[-1] - only(lane == LANES - 1, edge) - only(lane == LANES - 2, next_edge)
+        return tiles
+
     ends = (half // 2, half // 2 + half // 4)
-
-    def sums(side, held):
-        rows = slice(side * TILE, (side + 1) * TILE)
-        one, two, three = level_1[rows], level_2[rows], level_3[rows]
-        held[:, 0 : ends[0]] = one[:, 0 : ends[0]] + two
-        held[:, ends[0] : ends[1]] = one[:, ends[0] : ends[1]] + three
-        held[:, ends[1] :] = one[:, ends[1] :]
-
+    row = iota((TILE, LANES), 0)
+
+    def fill(held, one, two, three):
+        for number, value in enumerate(one):
+            if number < len(two) + len(three):
+                value = jnp.where(row < 4, (two + three)[number], value)
+            held[:, number * LANES : (number + 1) * LANES] = value
+
+    ends_3 = level_3([tile_of(2, b, 1) + tile_of(7, b, 1) for b in range(blocks)])
     to_target = pltpu.make_async_remote_copy(
         src_ref=message.at[0],
         dst_ref=received,
@@ -306,18 +374,23 @@
         device_id=partner,
         device_id_type=MESH,
     )
-    sums(0, message.at[0])
+    fill(message.at[0], level_1(0), level_2(0), ends_3)
 
     @pl.when(has_target)
     def _():
         to_target.start()
 
-    home[0 : 2 * TILE] = level_1[2 * TILE : 4 * TILE]
-    home[2 * TILE :, 0 : ends[0]] = level_2[2 * TILE : 3 * TILE]
-    home[2 * TILE :, ends[0] : ends[1]] = level_3[2 * TILE : 3 * TILE]
-    home[2 * TILE :, ends[1] :] = jnp.zeros((TILE, half - ends[1]), jnp.float32)
+    own_3 = level_3([tile_of(6, b, 1) for b in range(blocks)])
+    for band in range(2):
+        for number, value in enumerate(level_1(4 + band)):
+            home[band * TILE : (band + 1) * TILE, number * LANES : (number + 1) * LANES] = value
+    unused = [jnp.zeros((TILE, LANES), jnp.float32)] * 2
+    for number, value in enumerate(level_2(3) + own_3 + unused):
+        home[2 * TILE :, number * LANES : (number + 1) * LANES] = value
     to_partner.start()
-    sums(1, message.at[1])
+    fill(message.at[1], level_1(1), level_2(1), [])
+    for number, value in enumerate(ends_3):
+        third[:, number * LANES : (number + 1) * LANES] = value
     to_partner.wait_recv()
     pltpu.make_async_copy(merged, merged, sum_sem.at[0]).wait()
 
@@ -335,7 +408,7 @@
     for band in range(2):
         total = homed[band * TILE : (band + 1) * TILE]
         for side in range(2):
-            total = total + jnp.where(row == edges[side], spread(side, band, slice(0, half)), 0.0)
+            total = total + jnp.where(row == edges[side], spread(side, 4 + band, slice(0, half)), 0.0)
         out_1[band] = total
     row = iota((TILE, ends[0]), 0)
     total = homed[2 * TILE :, 0 : ends[0]]
@@ -343,13 +416,13 @@
         shift = 2 * (core if side == 0 else 1 - core)
         for number in range(4):
             target = number % 2 + 4 * (number // 2) + shift
-            total = total + jnp.where(row == target, spread(side, 2 + number, slice(0, ends[0])), 0.0)
+            total = total + jnp.where(row == target, spread(side, number, slice(0, ends[0])), 0.0)
     out_2[0] = total[0:4]
     out_2[1] = total[4:8]
-    third = slice(ends[0], ends[1])
-    total = homed[2 * TILE :, third] + sides[0][:, third] + sides[1][:, third]
-    out_3[0] = total[2:4]
-    out_3[1] = total[4:6]
+    last = slice(ends[0], ends[1])
+    total = homed[2 * TILE : 2 * TILE + 4, last] + homed[2 * TILE + 4 :, last] + received[0:4, last] + third[4:8]
+    out_3[0] = total[0:2]
+    out_3[1] = total[2:4]
 
     pltpu.make_async_copy(best, best, send_sem.at[0]).wait()
     pltpu.make_async_copy(merged, merged, send_sem.at[1]).wait()
@@ -382,7 +455,7 @@
     kept = [pltpu.VMEM(out.shape, out.dtype) for out in outs]
     pieces = [(0, start, half // 2) for start in range(0, width, half // 2)]
     pieces += [(slot, start, half) for slot in range(1, 4) for start in (0, half)]
-    table = row_weights(own)
+    row_table, column_table = row_weights(own), column_weights()
 
     def run(*refs):
         kernel(*refs, pieces=pieces)
@@ -390,31 +463,31 @@
     results = pl.pallas_call(
         run,
         out_shape=kept,
-        in_specs=[anywhere] * 5,
+        in_specs=[anywhere] * 6,
         out_specs=[whole] * 6,
         scratch_shapes=[
             pltpu.VMEM((4, 3, dates, chunk, width), jnp.int32),
             pltpu.VMEM((2, 3, chunk, width), jnp.int32),
             pltpu.VMEM((2, 3, chunk, width), jnp.int32),
             pltpu.VMEM((2, 3, chunk, width), jnp.int32),
-            pltpu.VMEM((8 * chunk, width + 2 * LANES), jnp.bfloat16),
-            pltpu.VMEM((8 * chunk, width // 2 + 2 * LANES), jnp.bfloat16),
-            pltpu.VMEM((8 * chunk, width // 4 + 2 * LANES), jnp.bfloat16),
+            pltpu.VMEM((2, 4 * chunk, width), jnp.bfloat16),
             pltpu.VMEM((2, TILE, half), jnp.float32),
             pltpu.VMEM((TILE, half), jnp.float32),
             pltpu.VMEM((3 * TILE, half), jnp.float32),
             pltpu.VMEM((3 * TILE, half), jnp.float32),
-            pltpu.VMEM(table.shape[1:], jnp.bfloat16),
+            pltpu.VMEM((TILE, half // 4), jnp.float32),
+            pltpu.VMEM(row_table.shape[1:], jnp.bfloat16),
+            pltpu.VMEM(column_table.shape, jnp.bfloat16),
             pltpu.SMEM((dates,), jnp.int32),
             pltpu.SemaphoreType.DMA((len(pieces),)),
-            pltpu.SemaphoreType.DMA((2,)),
+            pltpu.SemaphoreType.DMA((3,)),
             pltpu.SemaphoreType.DMA((4,)),
             pltpu.SemaphoreType.DMA((2, 2)),
             pltpu.SemaphoreType.DMA((3,)),
         ],
         compiler_params=pltpu.CompilerParams(collective_id=0, has_side_effects=True),
         name="composite",
-    )(red_band, nir_band, cloud_class, date_ordinal, jnp.asarray(table))
+    )(red_band, nir_band, cloud_class, date_ordinal, jnp.asarray(row_table), jnp.asarray(column_table))
     return pl.pallas_call(
         write_out,
         out_shape=outs,

time: 11.2 us -> 10.8 us (0.964)
  Pallas kernels: 10.4 us -> 9.97 us
    pallas_call x1, Pallas kernels: 9.6 us -> 9.15 us  [body(): pl.pallas_call(run, out_shape=kept, in_specs=[anywhere] * 6, out_specs=[w...]
where the time goes in v3:
time: 10.8 us; the launch traced here: 10.6 us
  Pallas kernels  9.97 us (92%)
  between operations  0.64 us (6%)
    pallas_call x1, Pallas kernels, body(): pl.pallas_call(run, out_shape=kept, in_specs=[anywhere] * 6, out_specs=[w...  9.15 us
    pallas_call x1, Pallas kernels, body(): pl.pallas_call(write_out, out_shape=outs, in_specs=[whole] * 6, out_specs...  0.82 us

profile of v3, /device:TPU:1, one launch (start us, length us, event | category | flops | bytes accessed | tf_op | source)
XLA Modules:
  0.0 10.6 jit_solution(17036859087934574082)
XLA Ops:
  0.6 9.2 %composite.1 = (s32[16,2048]{1,0:T(8,128)S(1)}, s32[16,2048]{1,0:T(8,128)S(1)}, s32[16,2048]{1,0:T(8,128)S(1)}, f32[2,8,1024]{2,1,0:T(8,128)S(1)}, f32[2,4,512]{2,1,0:T(4,128)S(1)}, /*index=5*/f32[2,2,256]{2,1,0:T(2,128)S(1)}) custom-call(s32[12,32,2048]{2,1,0:T(8,128)} %refs_0_.1, s32[12,32,2048]{2,1,0:T(8,128)} %refs_1_.1, s32[12,32,2048]{2,1,0:T(8,128)} %refs_2_.1, ...), custom_call_target="tpu_custom_call" | custom-call | tf_op jit(solution)/shard_map/composite/pallas_call | solution.py:463
  9.8 0.8 %write_out.1 = (s32[16,2048]{1,0:T(8,128)}, s32[16,2048]{1,0:T(8,128)}, s32[16,2048]{1,0:T(8,128)}, f32[2,8,1024]{2,1,0:T(8,128)}, f32[2,4,512]{2,1,0:T(4,128)}, /*index=5*/f32[2,2,256]{2,1,0:T(2,128)}) custom-call(s32[16,2048]{1,0:T(8,128)S(1)} %get-tuple-element.12.refs_0_, s32[16,2048]{1,0:T(8,128)S(1)} %get-tuple-element.13.refs_1_, ...), custom_call_target="tpu_custom_call" | custom-call | tf_op jit(solution)/shard_map/write_out/pallas_call | solution.py:491

commit v4 on v3

--- a/solution.py
+++ b/solution.py
@@ -15,6 +15,8 @@
 TILE = 8
 WIDTH = 512
 AT_2, AT_3 = 3, 71
+SENT = 6
+PIECES = ((0,512),(512,512),(1024,512),(1536,512))
 MESH = pl.DeviceIdType.MESH
 TAPS = np.array([1, 5, 10, 10, 5, 1], np.float64) / 32
 
@@ -27,10 +29,12 @@
     return value >> LIMB_BITS, value & LIMB_MASK
 
 
-def take_first(first, second):
+def take_first(first, second, earlier):
     r1a, r0a, n1a, n0a, clear_a, ord_a = first
     r1b, r0b, n1b, n0b, clear_b, ord_b = second
-    low = n0a * r0b - n0b * r0a + ((ord_b - ord_a) >> 31)
+    low = n0a * r0b - n0b * r0a
+    if not earlier:
+        low = low + ((ord_b - ord_a) >> 31)
     mid = (n1a * r0b + n0a * r1b) - (n1b * r0a + n0b * r1a) + (low >> LIMB_BITS)
     high = n1a * r1b - n1b * r1a + (mid >> LIMB_BITS)
     return high >= clear_b - clear_a
@@ -38,6 +42,26 @@
 
 def pick(take, first, second):
     return tuple(jnp.where(take, one, two) for one, two in zip(first, second))
+
+
+def sorted_scalars(keys):
+    keys, count = list(keys), len(keys)
+    top = 1
+    while 2 * top < count:
+        top *= 2
+    p = top
+    while p:
+        q, r, d = top, 0, p
+        while True:
+            for i in range(count - d):
+                if i & p == r:
+                    low, high = keys[i], keys[i + d]
+                    keys[i], keys[i + d] = jnp.minimum(low, high), jnp.maximum(low, high)
+            if q == p:
+                break
+            d, q, r = q - p, q // 2, p
+        p //= 2
+    return keys
 
 
 def joined(entry):
@@ -124,9 +148,9 @@
 
 
 def kernel(
-    red, nir, cloud, ordinals, row_table, column_table, out_red, out_nir, out_ord, out_1, out_2, out_3,
-    stream, best, arrived, merged, parts, message, received, home, homed, third, weights, columns_by,
-    ords, load_sem, order_sem, send_sem, best_sem, sum_sem, pieces,
+    red, nir, cloud, ordinals, table, out_red, out_nir, out_ord, out_1, out_2, out_3,
+    best, arrived, parts, message, outbox, beside, received, homed, third, weights,
+    ords, turns, load_sem, order_sem, send_sem, best_sem, sum_sem, *streams, pieces,
 ):
     tile = lax.axis_index("tiles")
     strip_index = lax.axis_index("rows")
@@ -144,26 +168,32 @@
     rows_of = [3 * core * chunk, (1 + core) * chunk, (3 - 3 * core) * chunk, (2 - core) * chunk]
 
     arrivals = []
-    for number, (slot, start, size) in enumerate(pieces):
+
+    def start_load(number):
+        slot, start, size = pieces[number]
+        semaphore = load_sem.at[number % load_sem.shape[0]]
         begin = pl.multiple_of(rows_of[slot], chunk)
         columns = pl.ds(start, size)
         for band, source in enumerate((red, nir, cloud)):
             pltpu.make_async_copy(
                 source.at[:, pl.ds(begin, chunk), columns],
-                stream.at[slot, band, :, :, columns],
-                load_sem.at[number],
+                streams[number].at[band],
+                semaphore,
             ).start()
-        whole = stream.at[slot, :, :, :, columns]
-        arrivals.append(pltpu.make_async_copy(whole, whole, load_sem.at[number]))
+        arrivals.append(pltpu.make_async_copy(streams[number], streams[number], semaphore))
+
+    def wait_load(number):
+        arrivals[number].wait()
+        if len(arrivals) < len(pieces):
+            start_load(len(arrivals))
+
+    for number in range(load_sem.shape[0]):
+        start_load(number)
     order_copy = pltpu.make_async_copy(ordinals, ords, order_sem.at[0])
     order_copy.start()
     case = 2 * (1 - core) + has_target.astype(jnp.int32)
-    table_copies = [
-        pltpu.make_async_copy(row_table.at[case], weights, order_sem.at[1]),
-        pltpu.make_async_copy(column_table, columns_by, order_sem.at[2]),
-    ]
-    for copy in table_copies:
-        copy.start()
+    table_copy = pltpu.make_async_copy(table.at[case], weights, order_sem.at[1])
+    table_copy.start()
 
     barrier = pltpu.get_barrier_semaphore()
     pl.semaphore_signal(barrier, inc=1, device_id=partner, device_id_type=MESH)
@@ -177,37 +207,46 @@
         received[...] = jnp.zeros(received.shape, jnp.float32)
 
     order_copy.wait()
-
-    def find_best(slot, start, size, own):
+    for number, key in enumerate(sorted_scalars([ords[date] * dates + date for date in range(dates)])):
+        turns[0, number] = key % dates
+        turns[1, number] = key // dates
+
+    def find_best(slot, start, size, own, stream, origin):
         place = slot - 2
+        wide = min(size, WIDTH)
 
         def step(number, unused):
-            at = pl.multiple_of(number * WIDTH + start, WIDTH)
-            columns = pl.ds(at, WIDTH)
-
-            def entry(date):
-                red_hi, red_lo = limbs(stream[slot, 0, date, :, columns])
-                nir_hi, nir_lo = limbs(stream[slot, 1, date, :, columns])
-                clear = jnp.where(stream[slot, 2, date, :, columns] == 0, FLAG, 0)
-                return (red_hi, red_lo, nir_hi, nir_lo, clear, ords[date])
+            at = pl.multiple_of(number * wide + start, wide)
+            columns = pl.ds(at, wide)
+            held = pl.ds(pl.multiple_of(at - origin, wide), wide)
+
+            def entry(turn):
+                date = turns[0, turn]
+                red_hi, red_lo = limbs(stream[0, date, :, held])
+                nir_hi, nir_lo = limbs(stream[1, date, :, held])
+                clear = jnp.where(stream[2, date, :, held] == 0, FLAG, 0)
+                return (red_hi, red_lo, nir_hi, nir_lo, clear, turns[1, turn])
+
+            def first_of(one, two, earlier):
+                return pick(take_first(one, two, earlier), one, two)
 
             current = None
+            for turn in range(0, dates, 2):
+                other = entry(turn)
+                if turn + 1 < dates:
+                    other = first_of(other, entry(turn + 1), True)
+                current = other if current is None else first_of(current, other, True)
             if own:
                 red_hi, red_lo = limbs(arrived[place, 0, :, columns])
                 nir_hi, nir_lo = limbs(arrived[place, 1, :, columns])
                 packed = arrived[place, 2, :, columns]
-                current = (red_hi, red_lo, nir_hi, nir_lo, packed & FLAG, packed & (FLAG - 1))
-            for date in range(0, dates, 2):
-                other = entry(date)
-                if date + 1 < dates:
-                    later = entry(date + 1)
-                    other = pick(take_first(later, other), later, other)
-                current = other if current is None else pick(take_first(other, current), other, current)
+                theirs = (red_hi, red_lo, nir_hi, nir_lo, packed & FLAG, packed & (FLAG - 1))
+                current = first_of(theirs, current, False)
             value_red, value_nir, clear, order = joined(current)
             if own:
-                merged[place, 0, :, columns] = value_red
-                merged[place, 1, :, columns] = value_nir
-                merged[place, 2, :, columns] = order
+                best[slot, 0, :, columns] = value_red
+                best[slot, 1, :, columns] = value_nir
+                best[slot, 2, :, columns] = order
                 both = jnp.concatenate([value_red, value_nir], axis=0).astype(jnp.float32)
                 high, low = split(both)
                 parts[0, place * 2 * chunk : (place + 1) * 2 * chunk, columns] = high
@@ -218,7 +257,7 @@
                 best[slot, 2, :, columns] = clear + order
             return unused
 
-        lax.fori_loop(0, size // WIDTH, step, 0)
+        lax.fori_loop(0, size // wide, step, 0, unroll=True)
 
     def best_copy(slot, part):
         columns = pl.ds(part * half, half)
@@ -231,16 +270,17 @@
             device_id_type=MESH,
         )
 
-    waiting = list(zip(pieces, arrivals))
+    waiting = list(enumerate(pieces))
 
     def run(slot, part):
         begin, end = part * half, (part + 1) * half
         at = begin
         while at < end:
-            if waiting and waiting[0][0][:2] == (slot, at):
-                waiting.pop(0)[1].wait()
-            stop = min([end] + [piece[1] for piece, _ in waiting if piece[0] == slot and piece[1] > at])
-            find_best(slot, at, stop - at, slot >= 2)
+            if waiting and waiting[0][1][:2] == (slot, at):
+                wait_load(waiting.pop(0)[0])
+            stop = min([end] + [piece[1] for _, piece in waiting if piece[0] == slot and piece[1] > at])
+            holder = max(n for n, piece in enumerate(pieces) if piece[0] == slot and piece[1] <= at)
+            find_best(slot, at, stop - at, slot >= 2, streams[holder], pieces[holder][1])
             at = stop
 
     for slot in range(2):
@@ -256,15 +296,14 @@
         merged_rows = pl.ds(pl.multiple_of(((1 - core) if slot == 0 else core) * chunk, chunk), chunk)
         for number, result in enumerate((out_red, out_nir, out_ord)):
             pltpu.make_async_remote_copy(
-                src_ref=merged.at[slot, number],
+                src_ref=best.at[slot + 2, number],
                 dst_ref=result.at[merged_rows],
-                send_sem=send_sem.at[1],
+                send_sem=send_sem.at[0],
                 recv_sem=sum_sem.at[0],
                 device_id=partner,
                 device_id_type=MESH,
             ).start()
-    for copy in table_copies:
-        copy.wait()
+    table_copy.wait()
 
     block = 2 * LANES
     blocks = width // block
@@ -277,15 +316,16 @@
         return jnp.dot(left, right, preferred_element_type=jnp.float32)
 
     high, low = stacked(0), stacked(1)
-    first = columns_by[:, 0:block]
+    base = 8 * TILE
+    first = jnp.concatenate([weights[base : base + block], weights[base + block : base + 2 * block]], axis=1)
     shares = product(high, first) + product(low, first)
-    second = product(high, columns_by[:, block : block + LANES])
+    second = product(high, weights[base + 2 * block : base + 3 * block])
     data = []
     for b in range(blocks):
         rows = slice(b * count, (b + 1) * count)
         for value in (shares[rows, 0:LANES], shares[rows, LANES:] + second[rows]):
             data.append(jnp.concatenate(split(value), axis=0))
-    sums = product(weights[:, 0 : 2 * count], jnp.concatenate(data, axis=1))
+    sums = product(weights[0:base, 0 : 2 * count], jnp.concatenate(data, axis=1))
     lane = iota((TILE, LANES), 1)
 
     def tile_of(number, b, half_of):
@@ -355,26 +395,26 @@
         for number, value in enumerate(one):
             if number < len(two) + len(three):
                 value = jnp.where(row < 4, (two + three)[number], value)
-            held[:, number * LANES : (number + 1) * LANES] = value
+            held[:, number * LANES : (number + 1) * LANES] = value[0:SENT]
 
     ends_3 = level_3([tile_of(2, b, 1) + tile_of(7, b, 1) for b in range(blocks)])
     to_target = pltpu.make_async_remote_copy(
-        src_ref=message.at[0],
+        src_ref=message,
         dst_ref=received,
-        send_sem=send_sem.at[2],
+        send_sem=send_sem.at[1],
         recv_sem=sum_sem.at[1],
         device_id=target,
         device_id_type=MESH,
     )
     to_partner = pltpu.make_async_remote_copy(
-        src_ref=home,
+        src_ref=outbox,
         dst_ref=homed,
-        send_sem=send_sem.at[3],
+        send_sem=send_sem.at[2],
         recv_sem=sum_sem.at[2],
         device_id=partner,
         device_id_type=MESH,
     )
-    fill(message.at[0], level_1(0), level_2(0), ends_3)
+    fill(message, level_1(0), level_2(0), ends_3)
 
     @pl.when(has_target)
     def _():
@@ -383,22 +423,22 @@
     own_3 = level_3([tile_of(6, b, 1) for b in range(blocks)])
     for band in range(2):
         for number, value in enumerate(level_1(4 + band)):
-            home[band * TILE : (band + 1) * TILE, number * LANES : (number + 1) * LANES] = value
+            outbox[band * TILE : (band + 1) * TILE, number * LANES : (number + 1) * LANES] = value
     unused = [jnp.zeros((TILE, LANES), jnp.float32)] * 2
     for number, value in enumerate(level_2(3) + own_3 + unused):
-        home[2 * TILE :, number * LANES : (number + 1) * LANES] = value
+        outbox[2 * TILE : 3 * TILE, number * LANES : (number + 1) * LANES] = value
     to_partner.start()
-    fill(message.at[1], level_1(1), level_2(1), [])
+    fill(beside, level_1(1), level_2(1), [])
     for number, value in enumerate(ends_3):
         third[:, number * LANES : (number + 1) * LANES] = value
     to_partner.wait_recv()
-    pltpu.make_async_copy(merged, merged, sum_sem.at[0]).wait()
+    pltpu.make_async_copy(best.at[0:2], best.at[0:2], sum_sem.at[0]).wait()
 
     @pl.when(has_source)
     def _():
         to_target.wait_recv()
 
-    sides = (received, message.at[1])
+    sides = (received, beside)
 
     def spread(side, row, columns):
         return jnp.broadcast_to(sides[side][row : row + 1, columns], (TILE, columns.stop - columns.start))
@@ -425,7 +465,7 @@
     out_3[1] = total[2:4]
 
     pltpu.make_async_copy(best, best, send_sem.at[0]).wait()
-    pltpu.make_async_copy(merged, merged, send_sem.at[1]).wait()
+
     to_partner.wait_send()
 
     @pl.when(has_target)
@@ -434,13 +474,11 @@
 
 
 def write_out(*refs):
+    *refs, amount, semaphore = refs
     count = len(refs) // 2
-    semaphores = refs[-1]
-    copies = [pltpu.make_async_copy(refs[n], refs[count + n], semaphores.at[n]) for n in range(count)]
-    for copy in copies:
-        copy.start()
-    for copy in copies:
-        copy.wait()
+    for n in range(count):
+        pltpu.make_async_copy(refs[n], refs[count + n], semaphore).start()
+    pltpu.make_async_copy(amount, amount, semaphore).wait()
 
 
 def body(red_band, nir_band, cloud_class, date_ordinal):
@@ -453,9 +491,13 @@
     outs = [jax.ShapeDtypeStruct((own, width), jnp.int32)] * 3
     outs += [jax.ShapeDtypeStruct((2, own >> n, width >> n), jnp.float32) for n in range(1, LEVELS + 1)]
     kept = [pltpu.VMEM(out.shape, out.dtype) for out in outs]
-    pieces = [(0, start, half // 2) for start in range(0, width, half // 2)]
+    pieces = [(0, start, size) for start, size in PIECES]
     pieces += [(slot, start, half) for slot in range(1, 4) for start in (0, half)]
-    row_table, column_table = row_weights(own), column_weights()
+    columns = column_weights()
+    columns = np.concatenate([columns[:, at : at + LANES] for at in range(0, 3 * LANES, LANES)], axis=0)
+    rows = row_weights(own)
+    table = np.concatenate([rows, np.broadcast_to(columns, (rows.shape[0], *columns.shape))], axis=1)
+    written = sum(out.size for out in outs)
 
     def run(*refs):
         kernel(*refs, pieces=pieces)
@@ -463,37 +505,37 @@
     results = pl.pallas_call(
         run,
         out_shape=kept,
-        in_specs=[anywhere] * 6,
+        in_specs=[anywhere] * 5,
         out_specs=[whole] * 6,
         scratch_shapes=[
-            pltpu.VMEM((4, 3, dates, chunk, width), jnp.int32),
-            pltpu.VMEM((2, 3, chunk, width), jnp.int32),
-            pltpu.VMEM((2, 3, chunk, width), jnp.int32),
+            pltpu.VMEM((4, 3, chunk, width), jnp.int32),
             pltpu.VMEM((2, 3, chunk, width), jnp.int32),
             pltpu.VMEM((2, 4 * chunk, width), jnp.bfloat16),
-            pltpu.VMEM((2, TILE, half), jnp.float32),
-            pltpu.VMEM((TILE, half), jnp.float32),
+            pltpu.VMEM((SENT, half), jnp.float32),
             pltpu.VMEM((3 * TILE, half), jnp.float32),
+            pltpu.VMEM((SENT, half), jnp.float32),
+            pltpu.VMEM((SENT, half), jnp.float32),
             pltpu.VMEM((3 * TILE, half), jnp.float32),
             pltpu.VMEM((TILE, half // 4), jnp.float32),
-            pltpu.VMEM(row_table.shape[1:], jnp.bfloat16),
-            pltpu.VMEM(column_table.shape, jnp.bfloat16),
+            pltpu.VMEM(table.shape[1:], jnp.bfloat16),
             pltpu.SMEM((dates,), jnp.int32),
-            pltpu.SemaphoreType.DMA((len(pieces),)),
+            pltpu.SMEM((2, dates), jnp.int32),
+            pltpu.SemaphoreType.DMA((7,)),
+            pltpu.SemaphoreType.DMA((2,)),
             pltpu.SemaphoreType.DMA((3,)),
-            pltpu.SemaphoreType.DMA((4,)),
             pltpu.SemaphoreType.DMA((2, 2)),
             pltpu.SemaphoreType.DMA((3,)),
+            *[pltpu.VMEM((3, dates, chunk, size), jnp.int32) for _, _, size in pieces],
         ],
         compiler_params=pltpu.CompilerParams(collective_id=0, has_side_effects=True),
         name="composite",
-    )(red_band, nir_band, cloud_class, date_ordinal, jnp.asarray(row_table), jnp.asarray(column_table))
+    )(red_band, nir_band, cloud_class, date_ordinal, jnp.asarray(table))
     return pl.pallas_call(
         write_out,
         out_shape=outs,
         in_specs=[whole] * 6,
         out_specs=[anywhere] * 6,
-        scratch_shapes=[pltpu.SemaphoreType.DMA((6,))],
+        scratch_shapes=[pltpu.VMEM((written // LANES, LANES), jnp.int32), pltpu.SemaphoreType.DMA],
         name="write_out",
     )(*[pltpu.with_memory_space_constraint(result, pltpu.VMEM) for result in results])
 

time: 10.8 us -> 10.5 us (0.972)
  Pallas kernels: 9.97 us -> 9.74 us
    pallas_call x1, Pallas kernels: 9.15 us -> 8.97 us  [body(): pl.pallas_call(run, out_shape=kept, in_specs=[anywhere] * 5, out_specs=[w...]
where the time goes in v4:
time: 10.5 us; the launch traced here: 10.4 us
  Pallas kernels  9.74 us (93%)
  between operations  0.64 us (6%)
    pallas_call x1, Pallas kernels, body(): pl.pallas_call(run, out_shape=kept, in_specs=[anywhere] * 5, out_specs=[w...  8.97 us
    pallas_call x1, Pallas kernels, body(): pl.pallas_call(write_out, out_shape=outs, in_specs=[whole] * 6, out_specs...  0.77 us

profile of v4, /device:TPU:1, one launch (start us, length us, event | category | flops | bytes accessed | tf_op | source)
XLA Modules:
  0.0 10.4 jit_solution(13468230664268048604)
XLA Ops:
  0.6 9.0 %composite.1 = (s32[16,2048]{1,0:T(8,128)S(1)}, s32[16,2048]{1,0:T(8,128)S(1)}, s32[16,2048]{1,0:T(8,128)S(1)}, f32[2,8,1024]{2,1,0:T(8,128)S(1)}, f32[2,4,512]{2,1,0:T(4,128)S(1)}, /*index=5*/f32[2,2,256]{2,1,0:T(2,128)S(1)}) custom-call(s32[12,32,2048]{2,1,0:T(8,128)} %refs_0_.1, s32[12,32,2048]{2,1,0:T(8,128)} %refs_1_.1, s32[12,32,2048]{2,1,0:T(8,128)} %refs_2_.1, ...), custom_call_target="tpu_custom_call" | custom-call | tf_op jit(solution)/shard_map/composite/pallas_call | solution.py:505
  9.6 0.8 %write_out.1 = (s32[16,2048]{1,0:T(8,128)}, s32[16,2048]{1,0:T(8,128)}, s32[16,2048]{1,0:T(8,128)}, f32[2,8,1024]{2,1,0:T(8,128)}, f32[2,4,512]{2,1,0:T(4,128)}, /*index=5*/f32[2,2,256]{2,1,0:T(2,128)}) custom-call(s32[16,2048]{1,0:T(8,128)S(1)} %get-tuple-element.12.refs_0_, s32[16,2048]{1,0:T(8,128)S(1)} %get-tuple-element.13.refs_1_, ...), custom_call_target="tpu_custom_call" | custom-call | tf_op jit(solution)/shard_map/write_out/pallas_call | solution.py:533

commit v5 on v4

--- a/solution.py
+++ b/solution.py
@@ -132,18 +132,18 @@
                     low = (beside == 0) == (side == 0)
                     rows = [[row if low else (own >> level + 1) - 1 - row for row in ends[level]] for level in range(LEVELS)]
                     rows = [sorted(some) for some in rows]
-                    put(beside * TILE + 4 + band, band, 1, rows[0][0])
+                    put(3 * beside * TILE + 4 + band, band, 1, rows[0][0])
                     for n in range(2):
-                        put(beside * TILE + 2 * band + n, band, 2, rows[1][n])
+                        put(3 * beside * TILE + 2 * band + n, band, 2, rows[1][n])
                         m = 4 * beside + 2 * band + n
-                        put(2 * TILE + m, band, 3, rows[2][n], 7 * TILE + m)
+                        put(TILE + m, band, 3, rows[2][n], 2 * TILE + m)
                 for row in range(own // 4):
-                    put(3 * TILE + band * (own // 4) + row, band, 2, row)
+                    put(4 * TILE + band * (own // 4) + row, band, 2, row)
                 for row in range(own // 2):
-                    put(4 * TILE + band * (own // 2) + row, band, 1, row)
+                    put(5 * TILE + band * (own // 2) + row, band, 1, row)
                 for row in range(own // 8):
                     m = band * (own // 8) + row
-                    put(6 * TILE + m, band, 3, row, 6 * TILE + 4 + m)
+                    put(7 * TILE + m, band, 3, row, 7 * TILE + 4 + m)
     return table.astype(jnp.bfloat16)
 
 
@@ -289,21 +289,26 @@
             if slot == 0 and part == 0:
                 pl.semaphore_wait(barrier, 1 + has_target.astype(jnp.int32))
             best_copy(slot, part).start()
-    for slot in range(2):
-        for part in range(2):
-            best_copy(slot, part).wait_recv()
-            run(slot + 2, part)
-        merged_rows = pl.ds(pl.multiple_of(((1 - core) if slot == 0 else core) * chunk, chunk), chunk)
+    def send_merged(place):
+        merged_rows = pl.ds(pl.multiple_of(((1 - core) if place == 0 else core) * chunk, chunk), chunk)
         for number, result in enumerate((out_red, out_nir, out_ord)):
             pltpu.make_async_remote_copy(
-                src_ref=best.at[slot + 2, number],
+                src_ref=best.at[place + 2, number],
                 dst_ref=result.at[merged_rows],
-                send_sem=send_sem.at[0],
+                send_sem=send_sem.at[3],
                 recv_sem=sum_sem.at[0],
                 device_id=partner,
                 device_id_type=MESH,
             ).start()
-    table_copy.wait()
+
+    for place in range(2):
+        for part in range(2):
+            best_copy(place, part).wait_recv()
+            if place == 1 and part == 1:
+                table_copy.wait()
+            run(place + 2, part)
+        if place == 0:
+            send_merged(place)
 
     block = 2 * LANES
     blocks = width // block
@@ -325,12 +330,14 @@
         rows = slice(b * count, (b + 1) * count)
         for value in (shares[rows, 0:LANES], shares[rows, LANES:] + second[rows]):
             data.append(jnp.concatenate(split(value), axis=0))
-    sums = product(weights[0:base, 0 : 2 * count], jnp.concatenate(data, axis=1))
+    data = jnp.concatenate(data, axis=1)
+    sums = [product(weights[0 : base // 2, 0 : 2 * count], data)]
     lane = iota((TILE, LANES), 1)
 
     def tile_of(number, b, half_of):
         at = b * block + half_of * LANES
-        return sums[number * TILE : (number + 1) * TILE, at : at + LANES]
+        row = (number % 4) * TILE
+        return sums[number // 4][row : row + TILE, at : at + LANES]
 
     def rolled(value, shift):
         return pltpu.roll(value, shift % LANES, 1)
@@ -397,7 +404,7 @@
                 value = jnp.where(row < 4, (two + three)[number], value)
             held[:, number * LANES : (number + 1) * LANES] = value[0:SENT]
 
-    ends_3 = level_3([tile_of(2, b, 1) + tile_of(7, b, 1) for b in range(blocks)])
+    ends_3 = level_3([tile_of(1, b, 1) + tile_of(2, b, 1) for b in range(blocks)])
     to_target = pltpu.make_async_remote_copy(
         src_ref=message,
         dst_ref=received,
@@ -420,15 +427,18 @@
     def _():
         to_target.start()
 
-    own_3 = level_3([tile_of(6, b, 1) for b in range(blocks)])
+    pltpu.make_async_copy(best.at[0:2], best.at[0:2], send_sem.at[0]).wait()
+    send_merged(1)
+    sums.append(product(weights[base // 2 : base, 0 : 2 * count], data))
+    own_3 = level_3([tile_of(7, b, 1) for b in range(blocks)])
     for band in range(2):
-        for number, value in enumerate(level_1(4 + band)):
+        for number, value in enumerate(level_1(5 + band)):
             outbox[band * TILE : (band + 1) * TILE, number * LANES : (number + 1) * LANES] = value
     unused = [jnp.zeros((TILE, LANES), jnp.float32)] * 2
-    for number, value in enumerate(level_2(3) + own_3 + unused):
+    for number, value in enumerate(level_2(4) + own_3 + unused):
         outbox[2 * TILE : 3 * TILE, number * LANES : (number + 1) * LANES] = value
     to_partner.start()
-    fill(beside, level_1(1), level_2(1), [])
+    fill(beside, level_1(3), level_2(3), [])
     for number, value in enumerate(ends_3):
         third[:, number * LANES : (number + 1) * LANES] = value
     to_partner.wait_recv()
@@ -464,7 +474,7 @@
     out_3[0] = total[0:2]
     out_3[1] = total[2:4]
 
-    pltpu.make_async_copy(best, best, send_sem.at[0]).wait()
+    pltpu.make_async_copy(best.at[2:4], best.at[2:4], send_sem.at[3]).wait()
 
     to_partner.wait_send()
 
@@ -522,7 +532,7 @@
             pltpu.SMEM((2, dates), jnp.int32),
             pltpu.SemaphoreType.DMA((7,)),
             pltpu.SemaphoreType.DMA((2,)),
-            pltpu.SemaphoreType.DMA((3,)),
+            pltpu.SemaphoreType.DMA((4,)),
             pltpu.SemaphoreType.DMA((2, 2)),
             pltpu.SemaphoreType.DMA((3,)),
             *[pltpu.VMEM((3, dates, chunk, size), jnp.int32) for _, _, size in pieces],

time: 10.5 us -> 10.4 us (level)
  Pallas kernels: 9.74 us -> 9.63 us
    pallas_call x1, Pallas kernels: 8.97 us -> 8.86 us  [body(): pl.pallas_call(run, out_shape=kept, in_specs=[anywhere] * 5, out_specs=[w...]
where the time goes in v5:
time: 10.4 us; the launch traced here: 10.3 us
  Pallas kernels  9.63 us (93%)
  between operations  0.64 us (6%)
    pallas_call x1, Pallas kernels, body(): pl.pallas_call(run, out_shape=kept, in_specs=[anywhere] * 5, out_specs=[w...  8.86 us
    pallas_call x1, Pallas kernels, body(): pl.pallas_call(write_out, out_shape=outs, in_specs=[whole] * 6, out_specs...  0.77 us

profile of v5, /device:TPU:1, one launch (start us, length us, event | category | flops | bytes accessed | tf_op | source)
XLA Modules:
  0.0 10.3 jit_solution(2944649532195667855)
XLA Ops:
  0.6 8.9 %composite.1 = (s32[16,2048]{1,0:T(8,128)S(1)}, s32[16,2048]{1,0:T(8,128)S(1)}, s32[16,2048]{1,0:T(8,128)S(1)}, f32[2,8,1024]{2,1,0:T(8,128)S(1)}, f32[2,4,512]{2,1,0:T(4,128)S(1)}, /*index=5*/f32[2,2,256]{2,1,0:T(2,128)S(1)}) custom-call(s32[12,32,2048]{2,1,0:T(8,128)} %refs_0_.1, s32[12,32,2048]{2,1,0:T(8,128)} %refs_1_.1, s32[12,32,2048]{2,1,0:T(8,128)} %refs_2_.1, ...), custom_call_target="tpu_custom_call" | custom-call | tf_op jit(solution)/shard_map/composite/pallas_call | solution.py:515
  9.5 0.8 %write_out.1 = (s32[16,2048]{1,0:T(8,128)}, s32[16,2048]{1,0:T(8,128)}, s32[16,2048]{1,0:T(8,128)}, f32[2,8,1024]{2,1,0:T(8,128)}, f32[2,4,512]{2,1,0:T(4,128)}, /*index=5*/f32[2,2,256]{2,1,0:T(2,128)}) custom-call(s32[16,2048]{1,0:T(8,128)S(1)} %get-tuple-element.12.refs_0_, s32[16,2048]{1,0:T(8,128)S(1)} %get-tuple-element.13.refs_1_, ...), custom_call_target="tpu_custom_call" | custom-call | tf_op jit(solution)/shard_map/write_out/pallas_call | solution.py:543
